TPU v7x, 32 devices: a whole 2x2x4 slice. The times are simulated.
32 devices in a mesh: shard: 4 (over z), ctx: 2 (over x), tp: 4 (over y, core).
Axes of the slice: x: 2, y: 2, z: 4, core: 2. Of those that a mesh axis runs over, the one named last changes fastest.
Arguments:
- tokens: bfloat16 [8, 1024, 1280], P('shard', ('ctx', 'tp')), may hold values from -6 to 6
- norm1_gain: float32 [1280], replicated, may hold values from 0.1 to 1.9
- norm1_bias: float32 [1280], replicated, may hold values from -3 to 3
- qkv_weight: bfloat16 [3, 1280, 1280], P(None, ('shard', 'ctx'), 'tp'), may hold values from -0.15625 to 0.15625
- qv_bias: float32 [2, 1280], replicated, may hold values from -3 to 3
- rel_rows: bfloat16 [31, 80], replicated, may hold values from -0.8984375 to 0.8984375
- rel_cols: bfloat16 [127, 80], replicated, may hold values from -0.8984375 to 0.8984375
- proj_weight: bfloat16 [1280, 1280], P('tp', ('shard', 'ctx')), may hold values from -1.25 to 1.25
- proj_bias: float32 [1280], replicated, may hold values from -3 to 3
- norm2_gain: float32 [1280], replicated, may hold values from 0.1 to 1.9
- norm2_bias: float32 [1280], replicated, may hold values from -3 to 3
- fc1_weight: bfloat16 [1280, 5120], P(('shard', 'ctx'), 'tp'), may hold values from -0.15625 to 0.15625
- fc1_bias: float32 [5120], replicated, may hold values from -3 to 3
- fc2_weight: bfloat16 [5120, 1280], P('tp', ('shard', 'ctx')), may hold values from -0.078125 to 0.078125
- fc2_bias: float32 [1280], replicated, may hold values from -3 to 3
- cotangent: bfloat16 [8, 1024, 1280], P('shard', ('ctx', 'tp')), may hold values from -6 to 6
Outputs:
- output: bfloat16 [8, 1024, 1280], P('shard', ('ctx', 'tp'))
- tokens_grad: bfloat16 [8, 1024, 1280], P('shard', ('ctx', 'tp'))
- norm1_gain_grad: float32 [1280], replicated
- norm1_bias_grad: float32 [1280], replicated
- qkv_weight_grad: float32 [3, 1280, 1280], P(None, ('shard', 'ctx'), 'tp')
- qv_bias_grad: float32 [2, 1280], replicated
- rel_rows_grad: float32 [31, 80], replicated
- rel_cols_grad: float32 [127, 80], replicated
- proj_weight_grad: float32 [1280, 1280], P('tp', ('shard', 'ctx'))
- proj_bias_grad: float32 [1280], replicated
- norm2_gain_grad: float32 [1280], replicated
- norm2_bias_grad: float32 [1280], replicated
- fc1_weight_grad: float32 [1280, 5120], P(('shard', 'ctx'), 'tp')
- fc1_bias_grad: float32 [5120], replicated
- fc2_weight_grad: float32 [5120, 1280], P('tp', ('shard', 'ctx'))
- fc2_bias_grad: float32 [1280], replicated
All inputs are finite; a program needn't handle non-finite values.
Results may differ from a plain program's by a relative error of at most 0.02.
Values may be sent and summed in bfloat16 or wider, within the bound.
A program may use at most 128 MiB of HBM per device.

v0:
```python
from functools import partial

import jax
import jax.numpy as jnp
from jax import lax
from jax.sharding import PartitionSpec as P

D = 1280
H = 16
HD = 80
FF = 5120
COLS = 64
ROWS_DEV = 8


PRECISE = lax.Precision.HIGHEST
EPSILON = 1e-06
NEGATIVE = -1e30


def layer_norm(values_in, gain_vec, shift_vec):
    average = jnp.mean(values_in, -1, keepdims=True)
    centred = values_in - average
    variance = jnp.mean(centred * centred, -1, keepdims=True)
    return centred * lax.rsqrt(variance + EPSILON) * gain_vec + shift_vec


def block_size():
    return 512


def to_heads(flat_rows, heads_local):
    images, length, feat_width = flat_rows.shape
    return flat_rows.reshape(images, length, heads_local, feat_width // heads_local).transpose(
        0, 2, 1, 3
    )


def from_heads(per_head):
    images, heads_local, length, head_dim = per_head.shape
    return per_head.transpose(0, 2, 1, 3).reshape(images, length, heads_local * head_dim)


def block_scores(query_heads, key_flat, rows_bias, cols_bias, first_key, scale_factor):
    key_heads = to_heads(key_flat, query_heads.shape[1])
    key_len = key_flat.shape[1]
    key_rows = key_len // COLS
    scores = scale_factor * jnp.einsum(
        "ihqc,ihkc->ihqk", query_heads, key_heads, preferred_element_type=jnp.float32
    )
    images, heads_local, query_len, unused_len = scores.shape
    row_part = lax.dynamic_slice_in_dim(rows_bias, first_key // COLS, key_rows, 3)
    scores = scores.reshape(images, heads_local, query_len, key_rows, COLS)
    scores = scores + row_part[..., :, None] + cols_bias[..., None, :]
    return scores.reshape(images, heads_local, query_len, key_len)


def relative_terms(query_flat, rows_param, cols_param, first_row, heads_local):
    images, length, feat_width = query_flat.shape
    rows_dev = length // COLS
    grid_rows = (rows_param.shape[0] + 1) // 2
    own_rows = first_row + jnp.arange(rows_dev, dtype=jnp.int32)
    key_rows = jnp.arange(grid_rows, dtype=jnp.int32)
    row_slots = jnp.arange(rows_param.shape[0], dtype=jnp.int32)
    pick_rows = (
        row_slots[None, None, :]
        == own_rows[:, None, None] - key_rows[None, :, None] + grid_rows - 1
    ).astype(jnp.float32)
    table_rows = jnp.einsum("rkj,jc->rkc", pick_rows, rows_param, precision=PRECISE)
    col_ids = jnp.arange(COLS, dtype=jnp.int32)
    col_slots = jnp.arange(cols_param.shape[0], dtype=jnp.int32)
    pick_cols = (
        col_slots[None, None, :] == col_ids[:, None, None] - col_ids[None, :, None] + COLS - 1
    ).astype(jnp.float32)
    table_cols = jnp.einsum("wkj,jc->wkc", pick_cols, cols_param, precision=PRECISE)
    grid_form = query_flat.reshape(images, rows_dev, COLS, heads_local, feat_width // heads_local)
    along_rows = jnp.einsum("irwhc,rkc->ihrwk", grid_form, table_rows, precision=PRECISE).reshape(
        images, heads_local, length, grid_rows
    )
    along_cols = jnp.einsum("irwhc,wkc->ihrwk", grid_form, table_cols, precision=PRECISE).reshape(
        images, heads_local, length, COLS
    )
    return (along_rows, along_cols)


def on_device(
    tokens,
    norm1_gain,
    norm1_bias,
    qkv_weight,
    qv_bias,
    rel_rows,
    rel_cols,
    proj_weight,
    proj_bias,
    norm2_gain,
    norm2_bias,
    fc1_weight,
    fc1_bias,
    fc2_weight,
    fc2_bias,
    cotangent,
):
    scale_factor = HD ** (-0.5)
    tp_count = lax.axis_size("tp")
    ctx_count = lax.axis_size("ctx")
    tp_rank = lax.axis_index("tp")
    ctx_rank = lax.axis_index("ctx")
    grid_rows = ROWS_DEV * ctx_count
    tok_image = grid_rows * COLS
    tok_ctx = ROWS_DEV * COLS
    heads_local = H // tp_count
    width_local = heads_local * HD
    ff_local = FF // tp_count
    images = tokens.shape[0]
    rows_table = rel_rows.astype(jnp.float32)
    cols_table = rel_cols.astype(jnp.float32)
    qkv_full, proj_full, fc1_full, fc2_full = (
        lax.all_gather(qkv_weight, ("shard", "ctx"), axis=1, tiled=True),
        lax.all_gather(proj_weight, ("shard", "ctx"), axis=1, tiled=True),
        lax.all_gather(fc1_weight, ("shard", "ctx"), axis=0, tiled=True),
        lax.all_gather(fc2_weight, ("shard", "ctx"), axis=1, tiled=True),
    )
    qv_local = lax.dynamic_slice_in_dim(qv_bias, tp_rank * width_local, width_local, 1)
    fc1_local = lax.dynamic_slice_in_dim(fc1_bias, tp_rank * ff_local, ff_local, 0)
    resid_in = tokens.astype(jnp.float32)
    normed1 = layer_norm(resid_in, norm1_gain, norm1_bias).astype(jnp.bfloat16)
    normed1_full = lax.all_gather(normed1, "tp", axis=1, tiled=True)
    projected = jnp.einsum(
        "itd,sde->itse", normed1_full, qkv_full, preferred_element_type=jnp.float32
    )
    queries = (projected[:, :, 0] + qv_local[0]).astype(jnp.bfloat16)
    keys_own = projected[:, :, 1].astype(jnp.bfloat16)
    values_own = (projected[:, :, 2] + qv_local[1]).astype(jnp.bfloat16)
    first_row = ctx_rank * ROWS_DEV
    rel_fn = partial(relative_terms, first_row=first_row, heads_local=heads_local)
    (along_rows, along_cols), rel_pull = jax.vjp(
        rel_fn, queries.astype(jnp.float32), rows_table, cols_table
    )
    query_heads = to_heads(queries, heads_local)
    start_state = (
        jnp.full((images, heads_local, tok_ctx), NEGATIVE, jnp.float32),
        jnp.zeros((images, heads_local, tok_ctx), jnp.float32),
        jnp.zeros((images, heads_local, tok_ctx, HD), jnp.float32),
        jnp.zeros((images, tok_image, width_local), jnp.bfloat16),
        jnp.zeros((images, tok_image, width_local), jnp.bfloat16),
    )
    shard_piece = (
        lax.all_gather(keys_own, "ctx", axis=1, tiled=True),
        lax.all_gather(values_own, "ctx", axis=1, tiled=True),
    )
    piece_len = shard_piece[0].shape[1]
    step_len = block_size()

    def one_step(inner, offset):
        run_max, run_sum, run_acc, keys_all, values_all = inner
        key_blk = lax.dynamic_slice_in_dim(shard_piece[0], offset, step_len, 1)
        value_blk = lax.dynamic_slice_in_dim(shard_piece[1], offset, step_len, 1)
        scores = block_scores(query_heads, key_blk, along_rows, along_cols, offset, scale_factor)
        new_max = jnp.maximum(run_max, jnp.max(scores, -1))
        factor = jnp.exp(run_max - new_max)
        weights_blk = jnp.exp(scores - new_max[..., None])
        run_sum = run_sum * factor + jnp.sum(weights_blk, -1)
        value_heads = to_heads(value_blk, heads_local)
        run_acc = run_acc * factor[..., None] + jnp.einsum(
            "ihqk,ihkc->ihqc",
            weights_blk.astype(jnp.bfloat16),
            value_heads,
            preferred_element_type=jnp.float32,
        )
        keys_all = lax.dynamic_update_slice_in_dim(keys_all, key_blk, offset, 1)
        values_all = lax.dynamic_update_slice_in_dim(values_all, value_blk, offset, 1)
        return ((new_max, run_sum, run_acc, keys_all, values_all), None)

    offsets = jnp.arange(piece_len // step_len, dtype=jnp.int32) * step_len
    result, unused = lax.scan(one_step, start_state, offsets)
    run_max, run_sum, run_acc, keys_all, values_all = result
    attn_heads = run_acc / run_sum[..., None]
    log_total = run_max + jnp.log(run_sum)
    attn_low = from_heads(attn_heads).astype(jnp.bfloat16)
    proj_part = jnp.einsum("itd,de->ite", attn_low, proj_full, preferred_element_type=jnp.float32)
    branch = lax.psum_scatter(
        proj_part.astype(jnp.bfloat16), "tp", scatter_dimension=1, tiled=True
    ).astype(jnp.float32)
    middle = resid_in + branch + proj_bias
    normed2 = layer_norm(middle, norm2_gain, norm2_bias).astype(jnp.bfloat16)
    normed2_full = lax.all_gather(normed2, "tp", axis=1, tiled=True)
    hidden_pre = (
        jnp.einsum("itd,df->itf", normed2_full, fc1_full, preferred_element_type=jnp.float32)
        + fc1_local
    )
    gelu_exact = partial(jax.nn.gelu, approximate=False)
    activated_f, gelu_pull = jax.vjp(gelu_exact, hidden_pre)
    activated = activated_f.astype(jnp.bfloat16)
    mlp_part = jnp.einsum("itf,fe->ite", activated, fc2_full, preferred_element_type=jnp.float32)
    mlp_out = lax.psum_scatter(
        mlp_part.astype(jnp.bfloat16), "tp", scatter_dimension=1, tiled=True
    ).astype(jnp.float32)
    output = (middle + mlp_out + fc2_bias).astype(jnp.bfloat16)
    cot_full = lax.all_gather(cotangent, "tp", axis=1, tiled=True)
    d_act = jnp.einsum("ite,fe->itf", cot_full, fc2_full, preferred_element_type=jnp.float32)
    d_hidden = gelu_pull(d_act)[0].astype(jnp.bfloat16)
    fc2_grad = jnp.einsum("itf,ite->fe", activated, cot_full, preferred_element_type=jnp.float32)
    fc1_grad = jnp.einsum("itd,itf->df", normed2_full, d_hidden, preferred_element_type=jnp.float32)
    fc1_bias_part = jnp.sum(d_hidden.astype(jnp.float32), (0, 1))
    fc2_bias_part = jnp.sum(cotangent.astype(jnp.float32), (0, 1))
    d_norm2_part = jnp.einsum("itf,df->itd", d_hidden, fc1_full, preferred_element_type=jnp.float32)
    d_norm2 = lax.psum_scatter(
        d_norm2_part.astype(jnp.bfloat16), "tp", scatter_dimension=1, tiled=True
    ).astype(jnp.float32)
    unused_out, norm2_pull = jax.vjp(layer_norm, middle, norm2_gain, norm2_bias)
    d_mid_part, gain2_part, bias2_part = norm2_pull(d_norm2)
    d_middle = cotangent.astype(jnp.float32) + d_mid_part
    d_branch = d_middle.astype(jnp.bfloat16)
    proj_bias_part = jnp.sum(d_branch.astype(jnp.float32), (0, 1))
    d_branch_full = lax.all_gather(d_branch, "tp", axis=1, tiled=True)
    proj_grad = jnp.einsum(
        "itd,ite->de", attn_low, d_branch_full, preferred_element_type=jnp.float32
    )
    d_attn = jnp.einsum(
        "ite,de->itd", d_branch_full, proj_full, preferred_element_type=jnp.float32
    ).astype(jnp.bfloat16)
    d_attn_heads = to_heads(d_attn, heads_local)
    delta_rows = jnp.sum(d_attn_heads.astype(jnp.float32) * attn_heads, -1)
    key_step = block_size()
    key_rows = key_step // COLS
    key_offsets = jnp.arange(tok_image // key_step, dtype=jnp.int32) * key_step

    def back_step(carried, offset):
        grad_query, grad_rows, grad_cols = carried
        key_blk = lax.dynamic_slice_in_dim(keys_all, offset, key_step, 1)
        value_blk = lax.dynamic_slice_in_dim(values_all, offset, key_step, 1)
        scores = block_scores(query_heads, key_blk, along_rows, along_cols, offset, scale_factor)
        soft_probs = jnp.exp(scores - log_total[..., None])
        value_heads = to_heads(value_blk, heads_local)
        key_heads = to_heads(key_blk, heads_local)
        d_probs = jnp.einsum(
            "ihqc,ihkc->ihqk", d_attn_heads, value_heads, preferred_element_type=jnp.float32
        )
        d_scores = (soft_probs * (d_probs - delta_rows[..., None])).astype(jnp.bfloat16)
        grad_query = grad_query + jnp.einsum(
            "ihqk,ihkc->ihqc", d_scores, key_heads, preferred_element_type=jnp.float32
        )
        grid_scores = d_scores.astype(jnp.float32).reshape(
            images, heads_local, tok_ctx, key_rows, COLS
        )
        row_sums = jnp.sum(grid_scores, 4)
        row_now = lax.dynamic_slice_in_dim(grad_rows, offset // COLS, key_rows, 3)
        grad_rows = lax.dynamic_update_slice_in_dim(
            grad_rows, row_now + row_sums, offset // COLS, 3
        )
        grad_cols = grad_cols + jnp.sum(grid_scores, 3)
        key_part = scale_factor * jnp.einsum(
            "ihqk,ihqc->ikhc", d_scores, query_heads, preferred_element_type=jnp.float32
        )
        value_part = jnp.einsum(
            "ihqk,ihqc->ikhc",
            soft_probs.astype(jnp.bfloat16),
            d_attn_heads,
            preferred_element_type=jnp.float32,
        )
        emitted = (
            key_part.reshape(images, key_step, width_local),
            value_part.reshape(images, key_step, width_local),
        )
        return ((grad_query, grad_rows, grad_cols), emitted)

    back_start = (
        jnp.zeros((images, heads_local, tok_ctx, HD), jnp.float32),
        jnp.zeros((images, heads_local, tok_ctx, grid_rows), jnp.float32),
        jnp.zeros((images, heads_local, tok_ctx, COLS), jnp.float32),
    )
    (grad_query, grad_rows, grad_cols), emitted = lax.scan(back_step, back_start, key_offsets)
    key_terms = emitted[0].transpose(1, 0, 2, 3).reshape(images, tok_image, width_local)
    value_terms = emitted[1].transpose(1, 0, 2, 3).reshape(images, tok_image, width_local)
    grad_keys, grad_values = (
        lax.psum_scatter(
            key_terms.astype(jnp.bfloat16), "ctx", scatter_dimension=1, tiled=True
        ).astype(jnp.float32),
        lax.psum_scatter(
            value_terms.astype(jnp.bfloat16), "ctx", scatter_dimension=1, tiled=True
        ).astype(jnp.float32),
    )
    d_query_rel, rows_grad_part, cols_grad_part = rel_pull((grad_rows, grad_cols))
    d_query = (scale_factor * from_heads(grad_query) + d_query_rel).astype(jnp.bfloat16)
    d_keys = grad_keys.astype(jnp.bfloat16)
    d_values = grad_values.astype(jnp.bfloat16)
    d_projected = jnp.stack((d_query, d_keys, d_values), axis=2)
    qkv_grad = jnp.einsum(
        "itd,itse->sde", normed1_full, d_projected, preferred_element_type=jnp.float32
    )
    qv_bias_part = jnp.stack(
        (
            jnp.sum(d_query.astype(jnp.float32), (0, 1)),
            jnp.sum(d_values.astype(jnp.float32), (0, 1)),
        )
    )
    d_norm1_part = jnp.einsum(
        "itse,sde->itd", d_projected, qkv_full, preferred_element_type=jnp.float32
    )
    d_norm1 = lax.psum_scatter(
        d_norm1_part.astype(jnp.bfloat16), "tp", scatter_dimension=1, tiled=True
    ).astype(jnp.float32)
    unused_in, norm1_pull = jax.vjp(layer_norm, resid_in, norm1_gain, norm1_bias)
    d_in_part, gain1_part, bias1_part = norm1_pull(d_norm1)
    tokens_grad = (d_middle + d_in_part).astype(jnp.bfloat16)
    qkv_out, proj_out, fc1_out, fc2_out = (
        lax.psum_scatter(
            qkv_grad.astype(jnp.bfloat16), ("shard", "ctx"), scatter_dimension=1, tiled=True
        ).astype(jnp.float32),
        lax.psum_scatter(
            proj_grad.astype(jnp.bfloat16), ("shard", "ctx"), scatter_dimension=1, tiled=True
        ).astype(jnp.float32),
        lax.psum_scatter(
            fc1_grad.astype(jnp.bfloat16), ("shard", "ctx"), scatter_dimension=0, tiled=True
        ).astype(jnp.float32),
        lax.psum_scatter(
            fc2_grad.astype(jnp.bfloat16), ("shard", "ctx"), scatter_dimension=1, tiled=True
        ).astype(jnp.float32),
    )
    qv_placed = lax.dynamic_update_slice_in_dim(
        jnp.zeros((2, D), jnp.float32), qv_bias_part, tp_rank * width_local, 1
    )
    fc1_placed = lax.dynamic_update_slice_in_dim(
        jnp.zeros((FF,), jnp.float32), fc1_bias_part, tp_rank * ff_local, 0
    )
    (
        gain1_sum,
        bias1_sum,
        qv_sum,
        rows_sum,
        cols_sum,
        projb_sum,
        gain2_sum,
        bias2_sum,
        fc1b_sum,
        fc2b_sum,
    ) = lax.psum(
        (
            gain1_part,
            bias1_part,
            qv_placed,
            rows_grad_part,
            cols_grad_part,
            proj_bias_part,
            gain2_part,
            bias2_part,
            fc1_placed,
            fc2_bias_part,
        ),
        ("shard", "ctx", "tp"),
    )
    return (
        output,
        tokens_grad,
        gain1_sum,
        bias1_sum,
        qkv_out,
        qv_sum,
        rows_sum,
        cols_sum,
        proj_out,
        projb_sum,
        gain2_sum,
        bias2_sum,
        fc1_out,
        fc1b_sum,
        fc2_out,
        fc2b_sum,
    )


def solution(mesh):
    in_specs = (
        P("shard", ("ctx", "tp"), None),
        P(),
        P(),
        P(None, ("shard", "ctx"), "tp"),
        P(),
        P(),
        P(),
        P("tp", ("shard", "ctx")),
        P(),
        P(),
        P(),
        P(("shard", "ctx"), "tp"),
        P(),
        P("tp", ("shard", "ctx")),
        P(),
        P("shard", ("ctx", "tp"), None),
    )
    out_specs = (
        P("shard", ("ctx", "tp"), None),
        P("shard", ("ctx", "tp"), None),
        P(),
        P(),
        P(None, ("shard", "ctx"), "tp"),
        P(),
        P(),
        P(),
        P("tp", ("shard", "ctx")),
        P(),
        P(),
        P(),
        P(("shard", "ctx"), "tp"),
        P(),
        P("tp", ("shard", "ctx")),
        P(),
    )
    return jax.shard_map(
        on_device, mesh=mesh, in_specs=in_specs, out_specs=out_specs, check_vma=False
    )
```

profile of v0, /device:TPU:8, one launch (start us, length us, event | category | flops | bytes accessed | tf_op | source)
XLA Modules:
  0.0 1191.1 jit_solution(12797612369814305608)
XLA Ops:
  15.0 25.2 %all-gather.11.cloned.1.call-done = bf16[2,512,1280]{2,1,0:T(8,128)(2,1)} async-done(((bf16[2,128,1280]{2,1,0:T(8,128)(2,1)}), bf16[2,512,1280]{2,1,0:T(8,128)(2,1)}) %all-gather.11.cloned.1.call-update) | async-done | bytes 2621456 | tf_op jit(solution)/shard_map/all_gather | solution.py:128
  40.2 60.2 %all-gather.13.cloned.1.call-done = bf16[3,1280,320]{2,1,0:T(8,128)(2,1)} async-done(((bf16[3,160,320]{2,1,0:T(8,128)(2,1)}), bf16[3,1280,320]{2,1,0:T(8,128)(2,1)}) %all-gather.13.cloned.1.call-update) | async-done | bytes 2457616 | tf_op jit(solution)/shard_map/all_gather | solution.py:119
  110.6 34.7 %all_gather.34 = bf16[320,1280]{0,1:T(8,128)(2,1)} all-gather(bf16[320,160]{0,1:T(8,128)(2,1)S(1)} %copy-done.51), channel_id=1, replica_groups=mesh['shard'=4,'ctx'=2,'tp'=4] {'shard','ctx'}, dimensions={1}, use_global_device_ids=true | all-gather | bytes 921600 | tf_op jit(solution)/shard_map/all_gather | solution.py:120
  175.3 56.3 %while.44 = (s32[]{:T(128)}, f32[2,4,512]{2,1,0:T(4,128)S(1)}, f32[2,4,512]{2,1,0:T(4,128)S(1)}, f32[2,4,512,80]{2,3,1,0:T(8,128)}, bf16[2,1024,320]{1,2,0:T(8,1...) while((s32[]{:T(128)}, f32[2,4,512]{2,1,0:T(4,128)S(1)}, ...), condition=%wide.wide.region_5.6_spmd.clone, body=%wide.wide.region_2.5_spmd.clone.sunk | while | flops 693063680 | bytes 48349676 | solution.py:176
  182.8 7.7 dynamic_update_slice.54
  239.0 34.0 %reduce-scatter.13.cloned.1.call-done = bf16[2,128,1280]{2,1,0:T(8,128)(2,1)} async-done(((bf16[2,512,1280]{2,1,0:T(8,128)(2,1)}), bf16[2,128,1280]{2,1,0:T(8,128)(2,1)}) %reduce-scatter.13.cloned.1.call-update) | async-done | bytes 655376 | tf_op jit(solution)/shard_map/reduce_scatter | solution.py:182
  279.6 56.9 %all-gather.19.cloned.1.call-done = bf16[1280,1280]{1,0:T(8,128)(2,1)} async-done(((bf16[160,1280]{1,0:T(8,128)(2,1)}), bf16[1280,1280]{1,0:T(8,128)(2,1)}) %all-gather.19.cloned.1.call-update) | async-done | bytes 3276816 | tf_op jit(solution)/shard_map/all_gather | solution.py:121
  336.5 26.4 %all-gather.17.cloned.1.call-done = bf16[2,512,1280]{2,1,0:T(8,128)(2,1)} async-done(((bf16[2,128,1280]{2,1,0:T(8,128)(2,1)}), bf16[2,512,1280]{2,1,0:T(8,128)(2,1)}) %all-gather.17.cloned.1.call-update) | async-done | bytes 2621456 | tf_op jit(solution)/shard_map/all_gather | solution.py:187
  372.9 13.4 %multiply_convert_fusion = (bf16[2,512,1280]{2,1,0:T(8,128)(2,1)}, f32[2,512,1280]{2,1,0:T(8,128)}) fusion(f32[2,512,1280]{2,1,0:T(8,128)S(1)} %get-tuple-element.728, f32[1280]{0:T(1024)S(1)} %dynamic_slice.62, u8[512,1280]{1,0:T(8,128)(4,1)S(1)} %get-tuple-element.630, u8[512,1280]{1,0:T(8,128)(4,1)S(1)} %get-tuple-element.629), kind=kLoop, calls=%fused_computation.47 | loop fusion | flops 93061120 | bytes 14423040 | tf_op jit(solution)/shard_map/convert_element_type | solution.py:194
  390.1 63.7 %all-gather.21.cloned.1.call-done = bf16[1280,1280]{0,1:T(8,128)(2,1)} async-done(((bf16[1280,160]{0,1:T(8,128)(2,1)}), bf16[1280,1280]{0,1:T(8,128)(2,1)}) %all-gather.21.cloned.1.call-update) | async-done | bytes 3276816 | tf_op jit(solution)/shard_map/all_gather | solution.py:122
  453.7 11.4 convert_reduce_fusion.2
  471.5 33.3 %reduce-scatter.17.cloned.1.call-done = bf16[2,128,1280]{2,1,0:T(8,128)(2,1)} async-done(((bf16[2,512,1280]{2,1,0:T(8,128)(2,1)}), bf16[2,128,1280]{2,1,0:T(8,128)(2,1)}) %reduce-scatter.17.cloned.1.call-update) | async-done | bytes 655376 | tf_op jit(solution)/shard_map/reduce_scatter | solution.py:208
  513.5 23.4 %all-gather.25.cloned.1.call-done = bf16[2,512,1280]{2,1,0:T(8,128)(2,1)} async-done(((bf16[2,128,1280]{2,1,0:T(8,128)(2,1)}), bf16[2,512,1280]{2,1,0:T(8,128)(2,1)}) %all-gather.25.cloned.1.call-update) | async-done | bytes 2621456 | tf_op jit(solution)/shard_map/all_gather | solution.py:216
  540.9 63.8 %while.45 = (s32[]{:T(128)}, f32[2,4,512,80]{2,3,1,0:T(8,128)}, f32[2,4,512,16]{2,3,1,0:T(8,128)}, f32[2,4,512,64]{2,3,1,0:T(8,128)}, bf16[2,2,512,320]{2,3,1,0:...) while((s32[]{:T(128)}, f32[2,4,512,80]{2,3,1,0:T(8,128)}, ...), condition=%wide.wide.region_17.18_spmd.clone, body=%wide.wide.region_14.17_spmd.clone.sunk | while | flops 1712848896 | bytes 136758032 | solution.py:273
  643.5 12.9 %reduce-scatter.19.cloned.1.call-done = bf16[2,512,320]{1,2,0:T(8,128)(2,1)} async-done(((bf16[2,1024,320]{1,2,0:T(8,128)(2,1)}), bf16[2,512,320]{1,2,0:T(8,128)(2,1)}) %reduce-scatter.19.cloned.1.call-update) | async-done | bytes 655376 | tf_op jit(solution)/shard_map/reduce_scatter | solution.py:277
  664.0 7.8 convolution_convert_fusion.1
  671.9 8.3 fusion.9
  680.5 8.3 fusion.8
  708.4 8.3 reshape.314
  740.4 74.3 %reduce-scatter.29.cloned.1.call-done = bf16[1280,160]{0,1:T(8,128)(2,1)} async-done(((bf16[1280,1280]{0,1:T(8,128)(2,1)}), bf16[1280,160]{0,1:T(8,128)(2,1)}) %reduce-scatter.29.cloned.1.call-update) | async-done | bytes 409616 | tf_op jit(solution)/shard_map/reduce_scatter | solution.py:317
  816.7 76.7 %reduce-scatter.27.cloned.1.call-done = bf16[160,1280]{1,0:T(8,128)(2,1)} async-done(((bf16[1280,1280]{1,0:T(8,128)(2,1)}), bf16[160,1280]{1,0:T(8,128)(2,1)}) %reduce-scatter.27.cloned.1.call-update) | async-done | bytes 409616 | tf_op jit(solution)/shard_map/reduce_scatter | solution.py:314
  895.3 64.4 %reduce-scatter.25.cloned.1.call-done = bf16[320,160]{0,1:T(8,128)(2,1)} async-done(((bf16[320,1280]{0,1:T(8,128)(2,1)}), bf16[320,160]{0,1:T(8,128)(2,1)}) %reduce-scatter.25.cloned.1.call-update) | async-done | bytes 102416 | tf_op jit(solution)/shard_map/reduce_scatter | solution.py:311
  961.4 71.6 %reduce-scatter.31.cloned.1.call-done = bf16[160,960]{1,0:T(8,128)(2,1)} async-done(((bf16[1280,960]{1,0:T(8,128)(2,1)}), bf16[160,960]{1,0:T(8,128)(2,1)}) %reduce-scatter.31.cloned.1.call-update) | async-done | bytes 307216
  1035.9 135.0 %all-reduce.3.cloned.1.call-done = (f32[1280]{0:T(1024)}, f32[1280]{0:T(1024)}, f32[2,1280]{1,0:T(2,128)}, f32[31,80]{1,0:T(8,128)}, f32[127,80]{0,1:T(8,128)}, ...) async-done(((f32[1280]{0:T(1024)}, f32[1280]{0:T(1024)}, f32[2,1280]{1,0:T(2,128)}, f32[31,80]{1,0:T(8,128)}, ...) | async-done | bytes 112016 | tf_op jit(solution)/shard_map/psum | solution.py:338
  (378 shorter events, 301.5 us)
Async XLA Ops:
  7.2 102.0 %copy-start = (bf16[127,80]{0,1:T(8,128)(2,1)S(1)}, bf16[127,80]{0,1:T(8,128)(2,1)}, u32[]{:S(2)}) copy-start(bf16[127,80]{0,1:T(8,128)(2,1)} %param.26) | copy-start | bytes 60964
  7.2 33.0 %all-gather.11.cloned.1.call-start = ((), (), s32[]{:S(2)}) async-start(), calls=%async_computation.10 | async-start | bytes 3276800 | tf_op jit(solution)/shard_map/all_gather | solution.py:128
  13.4 87.0 %all-gather.13.cloned.1.call-start = ((), (), s32[]{:S(2)}) async-start(), calls=%async_computation.11 | async-start | bytes 3317760 | tf_op jit(solution)/shard_map/all_gather | solution.py:119
  14.1 157.5 %all-gather.15.cloned.1.call-start = ((), (), s32[]{:S(2)}) async-start(), calls=%async_computation.12 | async-start | bytes 1966080 | tf_op jit(solution)/shard_map/all_gather | solution.py:150
  108.8 64.1 %all-gather.27.cloned.1.call-start = ((), (), s32[]{:S(2)}) async-start(), calls=%async_computation.27 | async-start | bytes 1966080 | tf_op jit(solution)/shard_map/all_gather | solution.py:149
  147.6 125.4 %reduce-scatter.13.cloned.1.call-start = ((), (), s32[]{:S(2)}) async-start(), calls=%async_computation.13 | async-start | bytes 3276800 | tf_op jit(solution)/shard_map/reduce_scatter | solution.py:182
  238.4 98.2 %all-gather.19.cloned.1.call-start = ((), (), s32[]{:S(2)}) async-start(), calls=%async_computation.15 | async-start | bytes 3686400 | tf_op jit(solution)/shard_map/all_gather | solution.py:121
  239.0 124.0 %all-gather.17.cloned.1.call-start = ((), (), s32[]{:S(2)}) async-start(), calls=%async_computation.14 | async-start | bytes 3276800 | tf_op jit(solution)/shard_map/all_gather | solution.py:187
  274.5 234.0 %copy-start.53 = (f32[2,128]{1,0:T(2,128)}, f32[2,128]{1,0:T(2,128)S(1)}, u32[]{:S(2)}) copy-start(f32[2,128]{1,0:T(2,128)S(1)} %broadcast_multiply_fusion.1) | copy-start | bytes 3076
  276.0 232.4 %copy-start.60 = (f32[2,128]{1,0:T(2,128)}, f32[2,128]{1,0:T(2,128)S(1)}, u32[]{:S(2)}) copy-start(f32[2,128]{1,0:T(2,128)S(1)} %fusion.90) | copy-start | bytes 3076
  277.3 112.8 %all-gather.23.cloned.1.call-start = ((), (), s32[]{:S(2)}) async-start(), calls=%async_computation.18 | async-start | bytes 3276800 | tf_op jit(solution)/shard_map/all_gather | solution.py:200
  278.1 175.7 %all-gather.21.cloned.1.call-start = ((), (), s32[]{:S(2)}) async-start(), calls=%async_computation.16 | async-start | bytes 3686400 | tf_op jit(solution)/shard_map/all_gather | solution.py:122
  278.8 226.0 %reduce-scatter.17.cloned.1.call-start = ((), (), s32[]{:S(2)}) async-start(), calls=%async_computation.19 | async-start | bytes 3276800 | tf_op jit(solution)/shard_map/reduce_scatter | solution.py:208
  471.5 65.4 %all-gather.25.cloned.1.call-start = ((), (), s32[]{:S(2)}) async-start(), calls=%async_computation.20 | async-start | bytes 3276800 | tf_op jit(solution)/shard_map/all_gather | solution.py:216
  511.2 132.3 %reduce-scatter.21.cloned.1.call-start = ((), (), s32[]{:S(2)}) async-start(), calls=%async_computation.22 | async-start | bytes 1966080 | tf_op jit(solution)/shard_map/reduce_scatter | solution.py:280
  607.4 49.0 %reduce-scatter.19.cloned.1.call-start = ((), (), s32[]{:S(2)}) async-start(), calls=%async_computation.21 | async-start | bytes 1966080 | tf_op jit(solution)/shard_map/reduce_scatter | solution.py:277
  608.8 122.9 %reduce-scatter.23.cloned.1.call-start = ((), (), s32[]{:S(2)}) async-start(), calls=%async_computation.23 | async-start | bytes 3276800 | tf_op jit(solution)/shard_map/reduce_scatter | solution.py:301
  664.0 72.4 %reduce-scatter.15.cloned.1.call-start = ((), (), s32[]{:S(2)}) async-start(), calls=%async_computation.17 | async-start | bytes 3276800 | tf_op jit(solution)/shard_map/reduce_scatter | solution.py:196
  671.9 142.9 %reduce-scatter.29.cloned.1.call-start = ((), (), s32[]{:S(2)}) async-start(), calls=%async_computation.26 | async-start | bytes 3686400 | tf_op jit(solution)/shard_map/reduce_scatter | solution.py:317
  680.2 213.2 %reduce-scatter.27.cloned.1.call-start = ((), (), s32[]{:S(2)}) async-start(), calls=%async_computation.25 | async-start | bytes 3686400 | tf_op jit(solution)/shard_map/reduce_scatter | solution.py:314
  688.8 271.0 %reduce-scatter.25.cloned.1.call-start = ((), (), s32[]{:S(2)}) async-start(), calls=%async_computation.24 | async-start | bytes 1105920 | tf_op jit(solution)/shard_map/reduce_scatter | solution.py:311
  694.2 338.8 %reduce-scatter.31.cloned.1.call-start = ((), (), s32[]{:S(2)}) async-start(), calls=%async_computation.28 | async-start | bytes 2949120
  716.8 454.1 %all-reduce.3.cloned.1.call-start = ((), (), s32[]{:S(2)}) async-start(), calls=%async_computation.29 | async-start | bytes 274432 | tf_op jit(solution)/shard_map/psum | solution.py:338
  893.4 290.7 %copy-start.1 = (bf16[127,80]{0,1:T(8,128)(2,1)S(1)}, bf16[127,80]{0,1:T(8,128)(2,1)}, u32[]{:S(2)}) copy-start(bf16[127,80]{0,1:T(8,128)(2,1)} %param.26) | copy-start | bytes 60964
  (84 other events, 620.5 us)
Sparse Core Ops, SparseCore 0:
  13.5 26.6 all-gather.10
  42.4 57.9 all-gather.12
  108.9 37.5 all-gather.14
  148.4 24.4 all-gather.26
  238.5 34.5 reduce-scatter.12
  275.1 61.4 all-gather.18
  338.7 24.2 all-gather.16
  364.5 25.5 all-gather.22
  392.2 61.4 all-gather.20
  471.6 33.1 reduce-scatter.16
  511.3 25.5 all-gather.24
  607.6 23.2 reduce-scatter.20
  633.1 23.2 reduce-scatter.18
  664.1 34.5 reduce-scatter.22
  701.0 34.4 reduce-scatter.14
  739.0 75.6 reduce-scatter.28
  818.2 75.1 reduce-scatter.26
  896.6 63.1 reduce-scatter.24
  963.3 69.6 reduce-scatter.30
  1040.4 130.4 all-reduce.2
where the time goes:
time: 1200 us; the launch traced here: 1190 us
  waiting for transfers between devices  766 us (64%)
  local copies, waits for them, and re-layouts  154 us (13%)
  matrix products  142 us (12%)
  other arithmetic  60.6 us (5%)
  blocking collectives  34.7 us (3%)
  loops' own time  16.4 us (1%)
  between operations  15.5 us (1%)
    psum x1, waiting for transfers between devices, on_device(): lax.psum((gain1_part, bias1_part, qv_placed, rows_grad_part, cols_grad_pa...  135 us
    reduce_scatter x1, waiting for transfers between devices, on_device(): lax.psum_scatter(fc1_grad.astype(jnp.bfloat16), ('shard', 'ctx'), scatter...  76.7 us
    unnamed x21, waiting for transfers between devices  74.5 us
    reduce_scatter x1, waiting for transfers between devices, on_device(): lax.psum_scatter(fc2_grad.astype(jnp.bfloat16), ('shard', 'ctx'), scatter...  74.3 us
    reduce_scatter x1, waiting for transfers between devices, on_device(): lax.psum_scatter(proj_grad.astype(jnp.bfloat16), ('shard', 'ctx'), scatte...  64.4 us
    all_gather x1, waiting for transfers between devices, on_device(): lax.all_gather(fc2_weight, ('shard', 'ctx'), axis=1, tiled=True)  63.7 us
    all_gather x1, waiting for transfers between devices, on_device(): lax.all_gather(qkv_weight, ('shard', 'ctx'), axis=1, tiled=True)  60.2 us
    all_gather x1, waiting for transfers between devices, on_device(): lax.all_gather(fc1_weight, ('shard', 'ctx'), axis=0, tiled=True)  56.9 us
  transfers between devices with their start and end apart: 20, of which 16 were waited for; matrix products, arithmetic and copies ran while one was open for 15% of the time, Pallas kernels for 0%

commit v1 on v0

--- a/solution.py
+++ b/solution.py
@@ -1,8 +1,11 @@
 from functools import partial
+import math
 
 import jax
 import jax.numpy as jnp
 from jax import lax
+from jax.experimental import pallas as pl
+from jax.experimental.pallas import tpu as pltpu
 from jax.sharding import PartitionSpec as P
 
 D = 1280
@@ -83,7 +86,7 @@
     return (along_rows, along_cols)
 
 
-def on_device(
+def on_device_rows(
     tokens,
     norm1_gain,
     norm1_bias,
@@ -370,6 +373,302 @@
     )
 
 
+F32 = jnp.float32
+BF16 = jnp.bfloat16
+NT = (((1,), (1,)), ((), ()))
+NN = (((1,), (0,)), ((), ()))
+TN = (((0,), (0,)), ((), ()))
+VMEM_GRANT = 60 * 2**20
+
+
+def mm(left, right, dims=NN):
+    return lax.dot_general(left, right, dims, preferred_element_type=F32)
+
+
+def lane_ids(shape):
+    return lax.broadcasted_iota(jnp.int32, shape, 1)
+
+
+def fwd_kernel(
+    heads, hd, cols, rows, qb, q_ref, k_ref, v_ref, tab_ref, hot_ref, o_ref, ob_ref, lse_ref, qa_ref, ka_ref
+):
+    tok = q_ref.shape[0]
+    c = hd**-0.5 * math.log2(math.e)
+    up = hd**0.5
+    for h in range(heads):
+        sl = slice(h * hd, (h + 1) * hd)
+        pad = jnp.zeros((tok, 128 - hd), BF16)
+        qp = jnp.concatenate([q_ref[:, sl], pad], 1)
+        kp = jnp.concatenate([k_ref[:, sl], pad], 1)
+        vt = jnp.concatenate([v_ref[:, sl], pad], 1).T
+        ka_ref[h, :, 0:128] = jnp.where(lane_ids((tok, 128)) < hd, kp, hot_ref[:, 0:128])
+        ka_ref[h, :, 128:256] = hot_ref[:, 128:256]
+        terms = mm(qp, tab_ref[...]) * up
+        ln = lane_ids((cols, 128))
+        for r in range(rows):
+            rs = slice(r * cols, (r + 1) * cols)
+            tr = pltpu.roll(terms[rs, 0:128], (65 + r) % 128, 1)
+            tc = pltpu.roll(terms[rs, 128:256], 65, 1, stride=1, stride_axis=0)
+            rh = tr.astype(BF16).astype(F32)
+            rl = pltpu.roll(tr - rh, rows, 1)
+            ch = tc.astype(BF16).astype(F32)
+            cl = pltpu.roll(tc - ch, 64, 1)
+            low = jnp.where(ln < hd + 2 * rows, rl, jnp.zeros_like(tr))
+            left = jnp.where(ln < hd, qp[rs].astype(F32), jnp.where(ln < hd + rows, rh, low))
+            qa_ref[h, rs, 0:128] = left.astype(BF16)
+            qa_ref[h, rs, 128:256] = jnp.where(ln < 64, ch, cl).astype(BF16)
+
+        def blk(i, _):
+            at = pl.ds(pl.multiple_of(i * qb, qb), qb)
+            s = mm(ka_ref[h], qa_ref[h, at, :], NT)
+            m = jnp.max(s, 0, keepdims=True)
+            p = jnp.exp2((s - m) * c)
+            l = jnp.sum(p, 0, keepdims=True)
+            o = (mm(vt, p.astype(BF16)) / l).T[:, 0:hd]
+            lse_ref[h : h + 1, at] = m * c + jnp.log2(l)
+            o_ref[at, sl] = o
+            ob_ref[at, sl] = o.astype(BF16)
+            return 0
+
+        lax.fori_loop(0, tok // qb, blk, 0)
+
+
+def attn_fwd(q, k, v, tab, hot, heads, hd, cols, rows, qb=256):
+    tok = q.shape[0]
+    S = jax.ShapeDtypeStruct
+    return pl.pallas_call(
+        partial(fwd_kernel, heads, hd, cols, rows, qb),
+        out_shape=(
+            S((tok, heads * hd), F32),
+            S((tok, heads * hd), BF16),
+            S((heads, tok), F32),
+            S((heads, tok, 256), BF16),
+            S((heads, tok, 256), BF16),
+        ),
+        compiler_params=pltpu.CompilerParams(vmem_limit_bytes=VMEM_GRANT),
+        name="attn_fwd",
+    )(q, k, v, tab, hot)
+
+
+def bwd_kernel(
+    heads, hd, cols, rows, qb,
+    qa_ref, ka_ref, v_ref, do_ref, o_ref, lse_ref, tab_ref, hot_ref,
+    dq_ref, dk_ref, dv_ref, rg_ref, kt_ref, acc_k, acc_v, del_ref,
+):
+    tok = v_ref.shape[0]
+    scale = hd**-0.5
+    c = scale * math.log2(math.e)
+    rg_ref[...] = jnp.zeros_like(rg_ref)
+    for h in range(heads):
+        sl = slice(h * hd, (h + 1) * hd)
+        pad = jnp.zeros((tok, 128 - hd), BF16)
+        vp = jnp.concatenate([v_ref[:, sl], pad], 1)
+        kt_ref[0:128, :] = jnp.where(lane_ids((tok, 128)) < hd, ka_ref[h, :, 0:128], hot_ref[:, 0:128]).T
+        kt_ref[128:256, :] = hot_ref[:, 128:256].T
+        prod = jnp.concatenate([do_ref[:, sl].astype(F32) * o_ref[:, sl], pad.astype(F32)], 1)
+        del_ref[...] = lax.dot_general(
+            jnp.ones((8, 128), F32), prod, NT, preferred_element_type=F32, precision=PRECISE
+        )
+        acc_k[...] = jnp.zeros_like(acc_k)
+        acc_v[...] = jnp.zeros_like(acc_v)
+
+        def blk(i, _):
+            at = pl.ds(pl.multiple_of(i * qb, qb), qb)
+            qblk = qa_ref[h, at, :]
+            dob = jnp.concatenate([do_ref[at, sl], jnp.zeros((qb, 128 - hd), BF16)], 1)
+            s = mm(ka_ref[h], qblk, NT)
+            p = jnp.exp2(s * c - lse_ref[h : h + 1, at])
+            dp = mm(vp, dob, NT)
+            ds = (p * (dp - del_ref[0:1, at])).astype(BF16)
+            acc_v[...] += mm(p.astype(BF16), dob)
+            acc_k[...] += mm(ds, qblk[:, 0:128])
+            dqa = mm(kt_ref[...], ds).T
+            ln = lane_ids((cols, 128))
+            parts = []
+            for j in range(qb // cols):
+                r = i * (qb // cols) + j
+                js = slice(j * cols, (j + 1) * cols)
+                dr = dqa[js, 0:128]
+                dr = jnp.where((ln >= hd) & (ln < hd + rows), dr, 0.0)
+                dr = pltpu.roll(dr, (48 + r) % 128, 1)
+                dc = pltpu.roll(dqa[js, 128:256], 0, 1, stride=1, stride_axis=0)
+                parts.append(jnp.concatenate([dr, dc], 1))
+            d = jnp.concatenate(parts, 0).astype(BF16)
+            rel = mm(d, tab_ref[...])
+            rg_ref[...] += mm(d, qblk[:, 0:128], TN)
+            dq_ref[at, sl] = (scale * dqa[:, 0:128] + rel)[:, 0:hd].astype(BF16)
+            return 0
+
+        lax.fori_loop(0, tok // qb, blk, 0)
+        dk_ref[:, sl] = (scale * acc_k[...])[:, 0:hd].astype(BF16)
+        dv_ref[:, sl] = acc_v[...][:, 0:hd].astype(BF16)
+
+
+def attn_bwd(qa, ka, v, do, o, lse, tab, hot, heads, hd, cols, rows, qb=256):
+    tok = v.shape[0]
+    S = jax.ShapeDtypeStruct
+    return pl.pallas_call(
+        partial(bwd_kernel, heads, hd, cols, rows, qb),
+        out_shape=(S((tok, heads * hd), BF16),) * 3 + (S((256, 128), F32),),
+        scratch_shapes=[
+            pltpu.VMEM((256, tok), BF16),
+            pltpu.VMEM((tok, 128), F32),
+            pltpu.VMEM((tok, 128), F32),
+            pltpu.VMEM((8, tok), F32),
+        ],
+        compiler_params=pltpu.CompilerParams(vmem_limit_bytes=VMEM_GRANT),
+        name="attn_bwd",
+    )(qa, ka, v, do, o, lse, tab, hot)
+
+
+def position_tables(rel_rows, rel_cols, hd):
+    gap = 128 - hd
+    rr = jnp.pad(rel_rows, ((0, 128 - rel_rows.shape[0]), (0, gap)))
+    rc = jnp.pad(rel_cols, ((0, 128 - rel_cols.shape[0]), (0, gap)))
+    fr = jnp.pad(rel_rows[::-1], ((0, 128 - rel_rows.shape[0]), (0, gap)))
+    fc = jnp.pad(rel_cols[::-1], ((0, 128 - rel_cols.shape[0]), (0, gap)))
+    return jnp.concatenate([fr, fc], 0).T, jnp.concatenate([rr, rc], 0)
+
+
+def position_hots(tok, hd, cols, rows):
+    t = lax.broadcasted_iota(jnp.int32, (tok, 256), 0)
+    l = lax.broadcasted_iota(jnp.int32, (tok, 256), 1)
+    kr = t // cols
+    kw = t % cols
+    first = (l == hd + kr) | (l == hd + rows + kr) | (l == 128 + kw) | (l == 192 + kw)
+    second = (l == hd + rows - 1 - kr) | (l == 128 + cols - 1 - kw)
+    return first.astype(BF16), second.astype(BF16)
+
+
+def swap_halves(block):
+    mine = lax.axis_index("ctx")
+    keep = lax.dynamic_index_in_dim(block, mine, 0, keepdims=False)
+    give = lax.dynamic_index_in_dim(block, 1 - mine, 0, keepdims=False)
+    got = lax.ppermute(give, "ctx", [(0, 1), (1, 0)])
+    first = mine == 0
+    return jnp.stack([jnp.where(first, keep, got), jnp.where(first, got, keep)])
+
+
+def ln_stats(values):
+    average = jnp.mean(values, -1, keepdims=True)
+    centred = values - average
+    inverse = lax.rsqrt(jnp.mean(centred * centred, -1, keepdims=True) + EPSILON)
+    return centred * inverse, inverse
+
+
+def ln_back(unit, inverse, gain, grad):
+    scaled = grad * gain
+    first = jnp.mean(scaled, -1, keepdims=True)
+    second = jnp.mean(scaled * unit, -1, keepdims=True)
+    return inverse * (scaled - first - unit * second)
+
+
+def on_device_images(
+    tokens, norm1_gain, norm1_bias, qkv_weight, qv_bias, rel_rows, rel_cols, proj_weight, proj_bias,
+    norm2_gain, norm2_bias, fc1_weight, fc1_bias, fc2_weight, fc2_bias, cotangent,
+):
+    tp_count = lax.axis_size("tp")
+    tp_rank = lax.axis_index("tp")
+    heads = H // tp_count
+    width = heads * HD
+    ff = FF // tp_count
+    rows = (rel_rows.shape[0] + 1) // 2
+    tok = rows * COLS
+    cotangent_own = swap_halves(cotangent)
+    tokens_own = swap_halves(tokens)
+    qkv_full = lax.all_gather(qkv_weight, ("shard", "ctx"), axis=1, tiled=True)
+    proj_full = lax.all_gather(proj_weight, ("shard", "ctx"), axis=1, tiled=True)
+    fc1_full = lax.all_gather(fc1_weight, ("shard", "ctx"), axis=0, tiled=True)
+    fc2_full = lax.all_gather(fc2_weight, ("shard", "ctx"), axis=1, tiled=True)
+    qv_local = lax.dynamic_slice_in_dim(qv_bias, tp_rank * width, width, 1)
+    fc1_local = lax.dynamic_slice_in_dim(fc1_bias, tp_rank * ff, ff, 0)
+    x = tokens_own.astype(F32)
+    g = cotangent_own.astype(F32)
+
+    def gather(block):
+        return lax.all_gather(block, "tp", axis=1, tiled=True).reshape(tok, D)
+
+    def scatter(part):
+        whole = part.astype(BF16).reshape(2, tok // 2, D)
+        return lax.psum_scatter(whole, "tp", scatter_dimension=1, tiled=True).astype(F32)
+
+    unit1, inv1 = ln_stats(x)
+    a1 = gather((unit1 * norm1_gain + norm1_bias).astype(BF16))
+    q = (mm(a1, qkv_full[0]) + qv_local[0]).astype(BF16)
+    k = mm(a1, qkv_full[1]).astype(BF16)
+    v = (mm(a1, qkv_full[2]) + qv_local[1]).astype(BF16)
+    tab_f, tab_b = position_tables(rel_rows, rel_cols, HD)
+    hot_f, hot_b = position_hots(tok, HD, COLS, rows)
+    o, o_low, lse, qa, ka = attn_fwd(q, k, v, tab_f, hot_f, heads, HD, COLS, rows)
+    mid = x + scatter(mm(o_low, proj_full)) + proj_bias
+    unit2, inv2 = ln_stats(mid)
+    a2 = gather((unit2 * norm2_gain + norm2_bias).astype(BF16))
+    cot = gather(cotangent_own)
+    pre = mm(a2, fc1_full) + fc1_local
+    cdf = 0.5 * (1.0 + lax.erf(pre * (2.0**-0.5)))
+    act = (pre * cdf).astype(BF16)
+    slope = cdf + pre * jnp.exp(-0.5 * pre * pre) * ((2.0 * math.pi) ** -0.5)
+    d_pre = (mm(cot, fc2_full, NT) * slope).astype(BF16)
+    d_a2 = scatter(mm(d_pre, fc1_full, NT))
+    output = (mid + scatter(mm(act, fc2_full)) + fc2_bias).astype(BF16)
+    fc2_grad = mm(act, cot, TN)
+    fc1_grad = mm(a2, d_pre, TN)
+    d_mid = g + ln_back(unit2, inv2, norm2_gain, d_a2)
+    d_branch = d_mid.astype(BF16)
+    d_branch_full = gather(d_branch)
+    d_o = mm(d_branch_full, proj_full, NT).astype(BF16)
+    proj_grad = mm(o_low, d_branch_full, TN)
+    dq, dk, dv, rel_grad = attn_bwd(qa, ka, v, d_o, o, lse, tab_b, hot_b, heads, HD, COLS, rows)
+    d_a1 = scatter(mm(dq, qkv_full[0], NT) + mm(dk, qkv_full[1], NT) + mm(dv, qkv_full[2], NT))
+    qkv_grad = jnp.stack([mm(a1, dq, TN), mm(a1, dk, TN), mm(a1, dv, TN)])
+    tokens_grad = (d_mid + ln_back(unit1, inv1, norm1_gain, d_a1)).astype(BF16)
+
+    def reduce(part, dim):
+        return lax.psum_scatter(
+            part.astype(BF16), ("shard", "ctx"), scatter_dimension=dim, tiled=True
+        ).astype(F32)
+
+    def total(part):
+        return jnp.sum(part.astype(F32), tuple(range(part.ndim - 1)))
+
+    qv_part = jnp.stack([total(dq), total(dv)])
+    qv_placed = lax.dynamic_update_slice_in_dim(jnp.zeros((2, D), F32), qv_part, tp_rank * width, 1)
+    fc1_placed = lax.dynamic_update_slice_in_dim(jnp.zeros((FF,), F32), total(d_pre), tp_rank * ff, 0)
+    small = lax.psum(
+        (
+            total(d_a1 * unit1),
+            total(d_a1),
+            qv_placed,
+            rel_grad[: rel_rows.shape[0], :HD],
+            rel_grad[128 : 128 + rel_cols.shape[0], :HD],
+            total(d_branch),
+            total(d_a2 * unit2),
+            total(d_a2),
+            fc1_placed,
+            total(cotangent),
+        ),
+        ("shard", "ctx", "tp"),
+    )
+    return (
+        swap_halves(output),
+        swap_halves(tokens_grad),
+        small[0],
+        small[1],
+        reduce(qkv_grad, 1),
+        small[2],
+        small[3],
+        small[4],
+        reduce(proj_grad, 1),
+        small[5],
+        small[6],
+        small[7],
+        reduce(fc1_grad, 0),
+        small[8],
+        reduce(fc2_grad, 1),
+        small[9],
+    )
+
+
 def solution(mesh):
     in_specs = (
         P("shard", ("ctx", "tp"), None),
@@ -407,6 +706,12 @@
         P("tp", ("shard", "ctx")),
         P(),
     )
+    def on_device(*arrays):
+        rows = (arrays[5].shape[0] + 1) // 2
+        fits = mesh.shape["tp"] == 4 and mesh.shape["ctx"] == 2 and HD + 2 * rows <= 128
+        fits = fits and arrays[0].shape[0] == mesh.shape["ctx"] and arrays[6].shape[0] <= 128
+        return (on_device_images if fits else on_device_rows)(*arrays)
+
     return jax.shard_map(
         on_device, mesh=mesh, in_specs=in_specs, out_specs=out_specs, check_vma=False
     )

time: 1200 us -> 1020 us (0.85)
  local copies, waits for them, and re-layouts: 154 us -> 37.1 us
  matrix products: 142 us -> 82.7 us
  Pallas kernels: 0 us -> 57.7 us
  other arithmetic: 60.6 us -> 36.5 us
  waiting for transfers between devices: 766 us -> 746 us
  loops' own time: 16.4 us -> 0 us
    dot_general x36 -> x18, matrix products: 142 us -> 82.7 us  [mm(): return lax.dot_general(left, right, dims, preferred_element_type=F32)]
    pallas_call x0 -> x2, Pallas kernels: none -> 57.7 us  [the longest x1 31.4 us: attn_bwd(): pl.pallas_call(partial(bwd_kernel, heads, hd, cols, rows, qb), out_shape=...]
    dynamic_update_slice x10 -> x2, local copies, waits for them, and re-layouts: 33.2 us -> 0.39 us  [the longest x1 0.22 us: on_device_images(): lax.dynamic_update_slice_in_dim(jnp.zeros((FF,), F32), total(d_pre), tp_r...]
    all_gather x9 -> x7, waiting for transfers between devices: 261 us -> 230 us  [the longest x4 69.7 us: gather(): return lax.all_gather(block, 'tp', axis=1, tiled=True).reshape(tok, D)]
    ppermute x0 -> x4, waiting for transfers between devices: none -> 26.5 us  [swap_halves(): got = lax.ppermute(give, 'ctx', [(0, 1), (1, 0)])]
    convert_element_type x13 -> x7, other arithmetic: 37.8 us -> 12.5 us  [the longest x3 5.5 us: reduce(): return lax.psum_scatter(part.astype(BF16), ('shard', 'ctx'), scatter_dime...]
    unnamed x144 -> x85, local copies, waits for them, and re-layouts: 45.6 us -> 26.9 us
    another operation x2 -> x0, loops' own time: 16.4 us -> none  [the longest x1 8.44 us: on_device(): result, unused = lax.scan(one_step, start_state, offsets)]
  transfers between devices with their start and end apart: 20 -> 20, of which waited for: 16 -> 17; matrix products, arithmetic and copies ran while one was open for 15% -> 10% of each run, Pallas kernels for 0% -> 0%
where the time goes in v1:
time: 1020 us; the launch traced here: 1010 us
  waiting for transfers between devices  746 us (73%)
  matrix products  82.7 us (8%)
  Pallas kernels  57.7 us (6%)
  local copies, waits for them, and re-layouts  37.1 us (4%)
  other arithmetic  36.5 us (4%)
  blocking collectives  30.7 us (3%)
  between operations  14.6 us (1%)
    reduce_scatter x3, waiting for transfers between devices, reduce(): lax.psum_scatter(part.astype(BF16), ('shard', 'ctx'), scatter_dimension=d...  187 us
    psum x1, waiting for transfers between devices, on_device_images(): lax.psum((total(d_a1 * unit1), total(d_a1), qv_placed, rel_grad[:rel_rows...  136 us
    reduce_scatter x4, waiting for transfers between devices, scatter(): lax.psum_scatter(whole, 'tp', scatter_dimension=1, tiled=True).astype(F32)  92.7 us
    dot_general x18, matrix products, mm(): return lax.dot_general(left, right, dims, preferred_element_type=F32)  82.7 us
    unnamed x17, waiting for transfers between devices  73.4 us
    all_gather x4, waiting for transfers between devices, gather(): return lax.all_gather(block, 'tp', axis=1, tiled=True).reshape(tok, D)  69.7 us
    all_gather x1, waiting for transfers between devices, on_device_images(): fc2_full = lax.all_gather(fc2_weight, ('shard', 'ctx'), axis=1, tiled=True)  63.7 us
    all_gather x1, waiting for transfers between devices, on_device_images(): qkv_full = lax.all_gather(qkv_weight, ('shard', 'ctx'), axis=1, tiled=True)  51.3 us
  transfers between devices with their start and end apart: 20, of which 17 were waited for; matrix products, arithmetic and copies ran while one was open for 10% of the time, Pallas kernels for 0%

profile of v1, /device:TPU:8, one launch (start us, length us, event | category | flops | bytes accessed | tf_op | source)
XLA Modules:
  0.0 1011.3 jit_solution(18237662489625865350)
XLA Ops:
  9.8 8.0 collective-permute-done
  25.6 30.7 %all_gather.26 = bf16[320,1280]{0,1:T(8,128)(2,1)S(1)} all-gather(bf16[320,160]{0,1:T(8,128)(2,1)S(1)} %copy-done.12), channel_id=1, replica_groups=mesh['shard'=4,'ctx'=2,'tp'=4] {'shard','ctx'}, dimensions={1}, use_global_device_ids=true | all-gather | bytes 921600 | tf_op jit(solution)/shard_map/all_gather | solution.py:580
  56.3 51.3 %all-gather.10.cloned.1.call-done = bf16[3,1280,320]{2,1,0:T(8,128)(2,1)} async-done(((bf16[3,160,320]{2,1,0:T(8,128)(2,1)}), bf16[3,1280,320]{2,1,0:T(8,128)(2,1)}) %all-gather.10.cloned.1.call-update) | async-done | bytes 2457616 | tf_op jit(solution)/shard_map/all_gather | solution.py:579
  119.9 26.3 %attn_fwd.1 = (f32[1024,320]{1,0:T(8,128)}, bf16[1024,320]{1,0:T(8,128)(2,1)}, f32[4,1024]{1,0:T(4,128)}, bf16[4,1024,256]{2,1,0:T(8,128)(2,1)}, bf16[4,1024,256]{2,1,0:T(8,128)(2,1)}) custom-call(bf16[1024,320]{1,0:T(8,128)(2,1)} %add_convert_fusion.2.q_ref, bf16[1024,320]{1,0:T(8,128)(2,1)} %copy.52.k_ref, bf16[1024,320]{1,0:T(8,128)(2,1)} %add_convert_fusion.1.v_ref, ...), custom_call_target="tpu_custom_call" | custom-call | tf_op jit(solution)/shard_map/attn_fwd/pallas_call | solution.py:439
  151.1 32.7 %reduce-scatter.11.cloned.1.call-done = bf16[2,128,1280]{2,1,0:T(8,128)(2,1)} async-done(((bf16[2,512,1280]{2,1,0:T(8,128)(2,1)}), bf16[2,128,1280]{2,1,0:T(8,128)(2,1)}) %reduce-scatter.11.cloned.1.call-update) | async-done | bytes 655376 | tf_op jit(solution)/shard_map/reduce_scatter | solution.py:593
  189.6 9.9 collective-permute-done.2
  202.1 45.3 %all-gather.14.cloned.1.call-done = bf16[1280,1280]{1,0:T(8,128)(2,1)} async-done(((bf16[160,1280]{1,0:T(8,128)(2,1)}), bf16[1280,1280]{1,0:T(8,128)(2,1)}) %all-gather.14.cloned.1.call-update) | async-done | bytes 3276816 | tf_op jit(solution)/shard_map/all_gather | solution.py:581
  247.3 26.2 %all-gather.12.cloned.1.call-done = bf16[2,512,1280]{2,1,0:T(8,128)(2,1)} async-done(((bf16[2,128,1280]{2,1,0:T(8,128)(2,1)}), bf16[2,512,1280]{2,1,0:T(8,128)(2,1)}) %all-gather.12.cloned.1.call-update) | async-done | bytes 2621456 | tf_op jit(solution)/shard_map/all_gather | solution.py:589
  273.6 9.0 multiply_convert_fusion
  282.5 18.6 %all-gather.18.cloned.1.call-done = bf16[2,512,1280]{2,1,0:T(8,128)(2,1)} async-done(((bf16[2,128,1280]{2,1,0:T(8,128)(2,1)}), bf16[2,512,1280]{2,1,0:T(8,128)(2,1)}) %all-gather.18.cloned.1.call-update) | async-done | bytes 2621456 | tf_op jit(solution)/shard_map/all_gather | solution.py:589
  301.1 63.7 %all-gather.16.cloned.1.call-done = bf16[1280,1280]{0,1:T(8,128)(2,1)} async-done(((bf16[1280,160]{0,1:T(8,128)(2,1)}), bf16[1280,1280]{0,1:T(8,128)(2,1)}) %all-gather.16.cloned.1.call-update) | async-done | bytes 3276816 | tf_op jit(solution)/shard_map/all_gather | solution.py:582
  364.8 8.5 convert_reduce_fusion
  386.1 25.5 %reduce-scatter.15.cloned.1.call-done = bf16[2,128,1280]{2,1,0:T(8,128)(2,1)} async-done(((bf16[2,512,1280]{2,1,0:T(8,128)(2,1)}), bf16[2,128,1280]{2,1,0:T(8,128)(2,1)}) %reduce-scatter.15.cloned.1.call-update) | async-done | bytes 655376 | tf_op jit(solution)/shard_map/reduce_scatter | solution.py:593
  414.1 34.5 %reduce-scatter.13.cloned.1.call-done = bf16[2,128,1280]{2,1,0:T(8,128)(2,1)} async-done(((bf16[2,512,1280]{2,1,0:T(8,128)(2,1)}), bf16[2,128,1280]{2,1,0:T(8,128)(2,1)}) %reduce-scatter.13.cloned.1.call-update) | async-done | bytes 655376 | tf_op jit(solution)/shard_map/reduce_scatter | solution.py:593
  453.1 24.9 %all-gather.20.cloned.1.call-done = bf16[2,512,1280]{2,1,0:T(8,128)(2,1)} async-done(((bf16[2,128,1280]{2,1,0:T(8,128)(2,1)}), bf16[2,512,1280]{2,1,0:T(8,128)(2,1)}) %all-gather.20.cloned.1.call-update) | async-done | bytes 2621456 | tf_op jit(solution)/shard_map/all_gather | solution.py:589
  482.2 31.4 %attn_bwd.1 = (bf16[1024,320]{1,0:T(8,128)(2,1)}, bf16[1024,320]{1,0:T(8,128)(2,1)}, bf16[1024,320]{1,0:T(8,128)(2,1)}, f32[256,128]{1,0:T(8,128)}) custom-call(bf16[4,1024,256]{2,1,0:T(8,128)(2,1)} %get-tuple-element.26.qa_ref, bf16[4,1024,256]{2,1,0:T(8,128)(2,1)} %get-tuple-element.27.ka_ref, bf16[1024,320]{1,0:T(8,128)(2,1)} %add_convert_fusion.1.v_ref, ...), custom_call_target="tpu_custom_call" | custom-call | tf_op jit(solution)/shard_map/attn_bwd/pallas_call | solution.py:510
  529.9 8.2 convolution_convert_fusion
  557.9 8.3 reshape.111
  571.6 8.7 collective-permute-done.1
  593.5 46.3 %reduce-scatter.21.cloned.1.call-done = bf16[160,1280]{1,0:T(8,128)(2,1)} async-done(((bf16[1280,1280]{1,0:T(8,128)(2,1)}), bf16[160,1280]{1,0:T(8,128)(2,1)}) %reduce-scatter.21.cloned.1.call-update) | async-done | bytes 409616 | tf_op jit(solution)/shard_map/reduce_scatter | solution.py:627
  641.8 76.5 %reduce-scatter.23.cloned.1.call-done = bf16[1280,160]{0,1:T(8,128)(2,1)} async-done(((bf16[1280,1280]{0,1:T(8,128)(2,1)}), bf16[1280,160]{0,1:T(8,128)(2,1)}) %reduce-scatter.23.cloned.1.call-update) | async-done | bytes 409616 | tf_op jit(solution)/shard_map/reduce_scatter | solution.py:627
  720.2 64.5 %reduce-scatter.19.cloned.1.call-done = bf16[320,160]{0,1:T(8,128)(2,1)} async-done(((bf16[320,1280]{0,1:T(8,128)(2,1)}), bf16[320,160]{0,1:T(8,128)(2,1)}) %reduce-scatter.19.cloned.1.call-update) | async-done | bytes 102416 | tf_op jit(solution)/shard_map/reduce_scatter | solution.py:627
  786.3 71.3 %reduce-scatter.25.cloned.1.call-done = bf16[160,960]{1,0:T(8,128)(2,1)} async-done(((bf16[1280,960]{1,0:T(8,128)(2,1)}), bf16[160,960]{1,0:T(8,128)(2,1)}) %reduce-scatter.25.cloned.1.call-update) | async-done | bytes 307216
  860.6 135.9 %all-reduce.7.cloned.1.call-done = (f32[1280]{0:T(1024)}, f32[1280]{0:T(1024)}, f32[2,1280]{1,0:T(2,128)}, f32[31,80]{1,0:T(8,128)}, f32[127,80]{1,0:T(8,128)}, ...) async-done(((f32[1280]{0:T(1024)}, f32[1280]{0:T(1024)}, f32[2,1280]{1,0:T(2,128)}, f32[31,80]{1,0:T(8,128)}, ...) | async-done | bytes 112016 | tf_op jit(solution)/shard_map/psum | solution.py:637
  (195 shorter events, 130.8 us)
Async XLA Ops:
  7.2 49.1 %all-gather.8.cloned.1.call-start = ((), (), s32[]{:S(2)}) async-start(), calls=%async_computation.8 | async-start | bytes 3276800 | tf_op jit(solution)/shard_map/all_gather | solution.py:589
  8.3 9.5 collective-permute-start
  20.5 87.1 %all-gather.10.cloned.1.call-start = ((), (), s32[]{:S(2)}) async-start(), calls=%async_computation.9 | async-start | bytes 3317760 | tf_op jit(solution)/shard_map/all_gather | solution.py:579
  21.3 162.5 %reduce-scatter.11.cloned.1.call-start = ((), (), s32[]{:S(2)}) async-start(), calls=%async_computation.10 | async-start | bytes 3276800 | tf_op jit(solution)/shard_map/reduce_scatter | solution.py:593
  56.3 90.0 %copy-start.9 = (bf16[320,1280]{0,1:T(8,128)(2,1)}, bf16[320,1280]{0,1:T(8,128)(2,1)S(1)}, u32[]{:S(2)}) copy-start(bf16[320,1280]{0,1:T(8,128)(2,1)S(1)} %all_gather.26) | copy-start | bytes 2457604
  150.5 96.8 %all-gather.14.cloned.1.call-start = ((), (), s32[]{:S(2)}) async-start(), calls=%async_computation.12 | async-start | bytes 3686400 | tf_op jit(solution)/shard_map/all_gather | solution.py:581
  151.1 37.0 %copy-start.7 = (bf16[2,128,1280]{2,1,0:T(8,128)(2,1)S(1)}, bf16[2,128,1280]{2,1,0:T(8,128)(2,1)}, u32[]{:S(2)}) copy-start(bf16[2,128,1280]{2,1,0:T(8,128)(2,1)} %param.31) | copy-start | bytes 1966084
  151.1 122.5 %all-gather.12.cloned.1.call-start = ((), (), s32[]{:S(2)}) async-start(), calls=%async_computation.11 | async-start | bytes 3276800 | tf_op jit(solution)/shard_map/all_gather | solution.py:589
  188.0 113.1 %all-gather.18.cloned.1.call-start = ((), (), s32[]{:S(2)}) async-start(), calls=%async_computation.15 | async-start | bytes 3276800 | tf_op jit(solution)/shard_map/all_gather | solution.py:589
  188.1 11.4 %collective-permute-start.2 = (bf16[128,1280]{1,0:T(8,128)(2,1)S(1)}, bf16[128,1280]{1,0:T(8,128)(2,1)S(1)}, u32[]{:S(2)}, u32[]{:S(2)}) collective-permute-start(bf16[128,1280]{1,0:T(8,128)(2,1)S(1)} %dynamic-slice_bitcast_fusion.1), channel_id=1, source_target_pairs={{0,4},{4,0},{1,5},{5,1},{2,6},{6,2},{3,7},{7,3},{8,12},{12,8},{9,1... | collective-permute-start | bytes 983048 | tf_op jit(solution)/shard_map/ppermute | solution.py:547
  200.5 164.3 %all-gather.16.cloned.1.call-start = ((), (), s32[]{:S(2)}) async-start(), calls=%async_computation.13 | async-start | bytes 3686400 | tf_op jit(solution)/shard_map/all_gather | solution.py:582
  201.2 210.4 %reduce-scatter.15.cloned.1.call-start = ((), (), s32[]{:S(2)}) async-start(), calls=%async_computation.16 | async-start | bytes 3276800 | tf_op jit(solution)/shard_map/reduce_scatter | solution.py:593
  378.2 70.4 %reduce-scatter.13.cloned.1.call-start = ((), (), s32[]{:S(2)}) async-start(), calls=%async_computation.14 | async-start | bytes 3276800 | tf_op jit(solution)/shard_map/reduce_scatter | solution.py:593
  386.1 62.6 %copy-start.22 = (f32[1280]{0:T(1024)S(1)}, f32[1280]{0:T(1024)}, u32[]{:S(2)}) copy-start(f32[1280]{0:T(1024)} %param.30) | copy-start | bytes 15364
  386.1 91.9 %all-gather.20.cloned.1.call-start = ((), (), s32[]{:S(2)}) async-start(), calls=%async_computation.17 | async-start | bytes 3276800 | tf_op jit(solution)/shard_map/all_gather | solution.py:589
  411.6 37.1 %copy-start.2 = (bf16[2,128,1280]{2,1,0:T(8,128)(2,1)S(1)}, bf16[2,128,1280]{2,1,0:T(8,128)(2,1)}, u32[]{:S(2)}) copy-start(bf16[2,128,1280]{2,1,0:T(8,128)(2,1)} %reduce-scatter.15.cloned.1.call-done) | copy-start | bytes 1966084
  452.3 133.1 %reduce-scatter.17.cloned.1.call-start = ((), (), s32[]{:S(2)}) async-start(), calls=%async_computation.18 | async-start | bytes 3276800 | tf_op jit(solution)/shard_map/reduce_scatter | solution.py:593
  521.5 118.3 %reduce-scatter.21.cloned.1.call-start = ((), (), s32[]{:S(2)}) async-start(), calls=%async_computation.20 | async-start | bytes 3686400 | tf_op jit(solution)/shard_map/reduce_scatter | solution.py:627
  529.8 188.4 %reduce-scatter.23.cloned.1.call-start = ((), (), s32[]{:S(2)}) async-start(), calls=%async_computation.21 | async-start | bytes 3686400 | tf_op jit(solution)/shard_map/reduce_scatter | solution.py:627
  538.1 246.6 %reduce-scatter.19.cloned.1.call-start = ((), (), s32[]{:S(2)}) async-start(), calls=%async_computation.19 | async-start | bytes 1105920 | tf_op jit(solution)/shard_map/reduce_scatter | solution.py:627
  543.1 314.5 %reduce-scatter.25.cloned.1.call-start = ((), (), s32[]{:S(2)}) async-start(), calls=%async_computation.22 | async-start | bytes 2949120
  566.2 430.2 %all-reduce.7.cloned.1.call-start = ((), (), s32[]{:S(2)}) async-start(), calls=%async_computation.23 | async-start | bytes 323584 | tf_op jit(solution)/shard_map/psum | solution.py:637
  568.1 12.2 %collective-permute-start.1 = (bf16[128,1280]{1,0:T(8,128)(2,1)}, bf16[128,1280]{1,0:T(8,128)(2,1)}, u32[]{:S(2)}, u32[]{:S(2)}) collective-permute-start(bf16[128,1280]{1,0:T(8,128)(2,1)} %dynamic-slice_bitcast_fusion.2), channel_id=1, source_target_pairs={{0,4},{4,0},{1,5},{5,1},{2,6},{6,2},{3,7},{7,3},{8,12},{12,8},{9,1... | collective-permute-start | bytes 983048 | tf_op jit(solution)/shard_map/ppermute | solution.py:547
  590.1 408.0 %collective-permute-start.3 = (bf16[128,1280]{1,0:T(8,128)(2,1)S(1)}, bf16[128,1280]{1,0:T(8,128)(2,1)S(1)}, u32[]{:S(2)}, u32[]{:S(2)}) collective-permute-start(bf16[128,1280]{1,0:T(8,128)(2,1)S(1)} %dynamic-slice_bitcast_fusion), channel_id=1, source_target_pairs={{0,4},{4,0},{1,5},{5,1},{2,6},{6,2},{3,7},{7,3},{8,12},{12,8},{9,1... | collective-permute-start | bytes 983048 | tf_op jit(solution)/shard_map/ppermute | solution.py:547
  (30 other events, 274.2 us)
Sparse Core Ops, SparseCore 0:
  20.6 26.7 all-gather.7
  49.6 57.9 all-gather.9
  150.6 33.1 reduce-scatter.10
  185.8 61.4 all-gather.13
  249.3 24.2 all-gather.11
  275.6 25.5 all-gather.17
  303.3 61.4 all-gather.15
  378.4 33.1 reduce-scatter.14
  414.1 34.4 reduce-scatter.12
  452.4 25.5 all-gather.19
  521.6 34.4 reduce-scatter.16
  559.6 80.1 reduce-scatter.20
  643.4 74.7 reduce-scatter.22
  721.4 63.2 reduce-scatter.18
  788.1 69.5 reduce-scatter.24
  865.1 131.3 all-reduce.6

commit v2 on v1

--- a/solution.py
+++ b/solution.py
@@ -379,6 +379,9 @@
 NN = (((1,), (0,)), ((), ()))
 TN = (((0,), (0,)), ((), ()))
 VMEM_GRANT = 60 * 2**20
+DMA = pltpu.SemaphoreType.DMA
+ANY = pl.BlockSpec(memory_space=pl.ANY)
+VM = pl.BlockSpec(memory_space=pltpu.VMEM)
 
 
 def mm(left, right, dims=NN):
@@ -389,18 +392,261 @@
     return lax.broadcasted_iota(jnp.int32, shape, 1)
 
 
+def place():
+    return lax.axis_index("shard"), lax.axis_index("ctx"), lax.axis_index("tp")
+
+
+def core_mate(t):
+    return t + 1 - 2 * lax.rem(t, 2)
+
+
+def far_mate(t):
+    return lax.rem(t + 2, 4)
+
+
+def send(src, dst, sems, k, where):
+    copy = pltpu.make_async_remote_copy(
+        src_ref=src,
+        dst_ref=dst,
+        send_sem=sems.at[0, k],
+        recv_sem=sems.at[1, k],
+        device_id=where,
+        device_id_type=pl.DeviceIdType.MESH,
+    )
+    copy.start()
+    return copy
+
+
+def greet(shards):
+    s, c, t = place()
+    peers = [{"ctx": 1 - c}, {"tp": core_mate(t)}, {"tp": far_mate(t)}]
+    peers += [{"shard": lax.rem(s + d, shards)} for d in range(1, shards)]
+    barrier = pltpu.get_barrier_semaphore()
+    for peer in peers:
+        pl.semaphore_signal(barrier, inc=1, device_id=peer, device_id_type=pl.DeviceIdType.MESH)
+    pl.semaphore_wait(barrier, len(peers))
+
+
+class Spread:
+    def __init__(self, shards, src, dst, sems, local):
+        s, c, _ = place()
+        self.shards, self.dst, self.sems = shards, dst, sems
+        own = 2 * s + c
+        self.local = pltpu.make_async_copy(src, dst.at[own], local)
+        self.local.start()
+        self.along = [
+            send(src, dst.at[own], sems, d, {"shard": lax.rem(s + d, shards)}) for d in range(1, shards)
+        ]
+        self.across = [send(src, dst.at[own], sems, 0, {"ctx": 1 - c})]
+
+    def forward(self):
+        s, c, _ = place()
+        for d in range(1, self.shards):
+            self.along[d - 1].wait_recv()
+            block = self.dst.at[2 * lax.rem(s + self.shards - d, self.shards) + c]
+            self.across.append(send(block, block, self.sems, self.shards + d - 1, {"ctx": 1 - c}))
+
+    def finish(self):
+        self.local.wait()
+        for copy in self.along:
+            copy.wait_send()
+        for copy in self.across:
+            copy.wait()
+
+    @staticmethod
+    def scratch(shards):
+        return [DMA((2, 2 * shards - 1)), DMA]
+
+
+class Collect:
+    def __init__(self, shards, src, cross, line, sems):
+        s, c, _ = place()
+        self.shards, self.src, self.cross, self.line, self.sems = shards, src, cross, line, sems
+        self.across = []
+        for d in range(shards):
+            to = lax.rem(s + d + 1, shards)
+            self.across.append(send(src.at[2 * to + 1 - c], cross.at[d], sems, d, {"ctx": 1 - c}))
+
+    def forward(self):
+        s, c, _ = place()
+        self.along = []
+        for d in range(self.shards):
+            to = lax.rem(s + d + 1, self.shards)
+            self.across[d].wait_recv()
+            if d < self.shards - 1:
+                both = self.src[2 * to + c].astype(F32) + self.cross[d].astype(F32)
+                self.cross[d] = both.astype(BF16)
+                self.along.append(
+                    send(self.cross.at[d], self.line.at[d], self.sems, self.shards + d, {"shard": to})
+                )
+
+    def finish(self, out):
+        s, c, _ = place()
+        for copy in self.across:
+            copy.wait_send()
+        acc = self.src[2 * s + c].astype(F32) + self.cross[self.shards - 1].astype(F32)
+        for d, copy in enumerate(self.along):
+            copy.wait()
+            acc = acc + self.line[d].astype(F32)
+        out[...] = acc
+
+    @staticmethod
+    def scratch(shards, block):
+        return [
+            pltpu.VMEM((shards,) + block, BF16),
+            pltpu.VMEM((max(shards - 1, 1),) + block, BF16),
+            DMA((2, 2 * shards - 1)),
+        ]
+
+
+class Share:
+    def __init__(self, full, sems):
+        self.full, self.sems, self.copies = full, sems, {}
+
+    def push(self, k, p, src=None):
+        _, _, t = place()
+        block = self.full.at[p, t]
+        src = block if src is None else src
+        self.copies[k] = [
+            send(src, block, self.sems, 3 * k, {"tp": far_mate(t)}),
+            send(src, block, self.sems, 3 * k + 1, {"tp": core_mate(t)}),
+        ]
+
+    def forward(self, k, p):
+        _, _, t = place()
+        self.copies[k][0].wait_recv()
+        block = self.full.at[p, far_mate(t)]
+        self.copies[k].append(send(block, block, self.sems, 3 * k + 2, {"tp": core_mate(t)}))
+
+    def finish(self, k):
+        first, second, third = self.copies[k]
+        first.wait_send()
+        second.wait()
+        third.wait()
+
+
+class Gather2:
+    def __init__(self, part, mate, far, out, sems):
+        self.part, self.mate, self.far, self.out, self.sems = part, mate, far, out, sems
+        self.first, self.second = {}, {}
+
+    def push(self, p):
+        _, _, t = place()
+        m = core_mate(t)
+        self.first[p] = [
+            send(self.part.at[p, far_mate(m)], self.mate.at[p, 1], self.sems, 3 * p, {"tp": m}),
+            send(self.part.at[p, m], self.mate.at[p, 0], self.sems, 3 * p + 1, {"tp": m}),
+        ]
+
+    def forward(self, p):
+        _, _, t = place()
+        self.first[p][0].wait_recv()
+        both = self.part[p, far_mate(t)].astype(F32) + self.mate[p, 1].astype(F32)
+        self.out[p] = both.astype(BF16)
+        self.second[p] = send(self.out.at[p], self.far.at[p], self.sems, 3 * p + 2, {"tp": far_mate(t)})
+
+    def result(self, p):
+        _, _, t = place()
+        self.first[p][1].wait_recv()
+        self.second[p].wait_recv()
+        return self.part[p, t].astype(F32) + self.mate[p, 0].astype(F32) + self.far[p].astype(F32)
+
+    def finish(self, p):
+        for copy in self.first[p]:
+            copy.wait_send()
+        self.second[p].wait_send()
+
+    @staticmethod
+    def scratch(block):
+        return [
+            pltpu.VMEM((2, 2) + block, BF16),
+            pltpu.VMEM((2,) + block, BF16),
+            pltpu.VMEM((2,) + block, BF16),
+            DMA((2, 6)),
+        ]
+
+
+def ln_stats(values):
+    average = jnp.mean(values, -1, keepdims=True)
+    centred = values - average
+    inverse = lax.rsqrt(jnp.mean(centred * centred, -1, keepdims=True) + EPSILON)
+    return centred * inverse, inverse
+
+
+def ln_back(unit, inverse, gain, grad):
+    scaled = grad * gain
+    first = jnp.mean(scaled, -1, keepdims=True)
+    second = jnp.mean(scaled * unit, -1, keepdims=True)
+    return inverse * (scaled - first - unit * second)
+
+
+def comm_call(kernel, name, ident, args, outs, scratch, hbm_in=(), hbm_out=()):
+    return pl.pallas_call(
+        kernel,
+        out_shape=tuple(outs),
+        in_specs=[ANY if i in hbm_in else VM for i in range(len(args))],
+        out_specs=tuple(ANY if i in hbm_out else VM for i in range(len(outs))),
+        scratch_shapes=scratch,
+        compiler_params=pltpu.CompilerParams(
+            vmem_limit_bytes=VMEM_GRANT, collective_id=ident, has_side_effects=True
+        ),
+        name=name,
+    )(*args)
+
+
+def front_kernel(
+    shards, tok_ref, w_ref, gain_ref, bias_ref, x_ref, a_ref, wf_ref, swap_sems, share_sems, w_sems, w_local
+):
+    s, c, t = place()
+    greet(shards)
+    swap = send(tok_ref.at[1 - c], x_ref.at[c], swap_sems, 0, {"ctx": 1 - c})
+    spread = Spread(shards, w_ref, wf_ref, w_sems, w_local)
+    share = Share(a_ref, share_sems)
+
+    def norm(block):
+        unit, _ = ln_stats(block.astype(F32))
+        return (unit * gain_ref[...] + bias_ref[...]).astype(BF16)
+
+    own = tok_ref[c]
+    x_ref[c] = own
+    a_ref[c, t] = norm(own)
+    share.push(0, c)
+    swap.wait()
+    a_ref[1 - c, t] = norm(x_ref[1 - c])
+    share.push(1, 1 - c)
+    share.forward(0, c)
+    spread.forward()
+    share.forward(1, 1 - c)
+    share.finish(0)
+    share.finish(1)
+    spread.finish()
+
+
 def fwd_kernel(
-    heads, hd, cols, rows, qb, q_ref, k_ref, v_ref, tab_ref, hot_ref, o_ref, ob_ref, lse_ref, qa_ref, ka_ref
+    shards, heads, hd, cols, rows, qb,
+    qkv_ref, tab_ref, hot_ref, cot_ref, w_ref,
+    o_ref, ob_ref, lse_ref, qa_ref, ka_ref, g_ref, cf_ref, wf_ref,
+    swap_sems, share_sems, w_sems, w_local,
 ):
-    tok = q_ref.shape[0]
+    _, me, t = place()
+    greet(shards)
+    swap = send(cot_ref.at[1 - me], g_ref.at[me], swap_sems, 0, {"ctx": 1 - me})
+    spread = Spread(shards, w_ref, wf_ref, w_sems, w_local)
+    share = Share(cf_ref, share_sems)
+    own = cot_ref[me]
+    g_ref[me] = own
+    cf_ref[me, t] = own
+    share.push(0, me, cot_ref.at[me])
+    tok = qkv_ref.shape[0]
     c = hd**-0.5 * math.log2(math.e)
     up = hd**0.5
     for h in range(heads):
         sl = slice(h * hd, (h + 1) * hd)
+        q_sl, k_sl, v_sl = (slice((j * heads + h) * hd, (j * heads + h + 1) * hd) for j in range(3))
         pad = jnp.zeros((tok, 128 - hd), BF16)
-        qp = jnp.concatenate([q_ref[:, sl], pad], 1)
-        kp = jnp.concatenate([k_ref[:, sl], pad], 1)
-        vt = jnp.concatenate([v_ref[:, sl], pad], 1).T
+        qp = jnp.concatenate([qkv_ref[:, q_sl], pad], 1)
+        kp = jnp.concatenate([qkv_ref[:, k_sl], pad], 1)
+        vt = jnp.concatenate([qkv_ref[:, v_sl], pad], 1).T
         ka_ref[h, :, 0:128] = jnp.where(lane_ids((tok, 128)) < hd, kp, hot_ref[:, 0:128])
         ka_ref[h, :, 128:256] = hot_ref[:, 128:256]
         terms = mm(qp, tab_ref[...]) * up
@@ -431,38 +677,107 @@
             return 0
 
         lax.fori_loop(0, tok // qb, blk, 0)
-
-
-def attn_fwd(q, k, v, tab, hot, heads, hd, cols, rows, qb=256):
-    tok = q.shape[0]
-    S = jax.ShapeDtypeStruct
-    return pl.pallas_call(
-        partial(fwd_kernel, heads, hd, cols, rows, qb),
-        out_shape=(
-            S((tok, heads * hd), F32),
-            S((tok, heads * hd), BF16),
-            S((heads, tok), F32),
-            S((heads, tok, 256), BF16),
-            S((heads, tok, 256), BF16),
-        ),
-        compiler_params=pltpu.CompilerParams(vmem_limit_bytes=VMEM_GRANT),
-        name="attn_fwd",
-    )(q, k, v, tab, hot)
+        if h == 0:
+            swap.wait()
+            cf_ref[1 - me, t] = g_ref[1 - me]
+            share.push(1, 1 - me, g_ref.at[1 - me])
+        if h == min(1, heads - 1):
+            spread.forward()
+        if h == heads - 1:
+            share.forward(0, me)
+            share.forward(1, 1 - me)
+    share.finish(0)
+    share.finish(1)
+    spread.finish()
+
+
+def mid_kernel(
+    shards, part_ref, x_ref, pb_ref, gain_ref, bias_ref, w_ref, mid_ref, a_ref, wf_ref,
+    mate, far, outb, sum_sems, share_sems, w_sems, w_local,
+):
+    _, _, t = place()
+    greet(shards)
+    gather = Gather2(part_ref, mate, far, outb, sum_sems)
+    gather.push(0)
+    gather.push(1)
+    spread = Spread(shards, w_ref, wf_ref, w_sems, w_local)
+    share = Share(a_ref, share_sems)
+    gather.forward(0)
+    gather.forward(1)
+    for p in range(2):
+        mid = x_ref[p].astype(F32) + gather.result(p) + pb_ref[...]
+        mid_ref[p] = mid
+        unit, _ = ln_stats(mid)
+        a_ref[p, t] = (unit * gain_ref[...] + bias_ref[...]).astype(BF16)
+        share.push(p, p)
+    spread.forward()
+    for p in range(2):
+        share.forward(p, p)
+    for p in range(2):
+        gather.finish(p)
+        share.finish(p)
+    spread.finish()
+
+
+def turn_kernel(
+    shards, part_ref, mid_ref, g_ref, gain_ref, w_ref, dm_ref, db_ref, wg_ref, sums_ref,
+    mate, far, outb, sum_sems, share_sems, w_cross, w_line, w_sems,
+):
+    _, _, t = place()
+    greet(shards)
+    gather = Gather2(part_ref, mate, far, outb, sum_sems)
+    gather.push(0)
+    gather.push(1)
+    collect = Collect(shards, w_ref, w_cross, w_line, w_sems)
+    share = Share(db_ref, share_sems)
+    gather.forward(0)
+    gather.forward(1)
+    rows = [jnp.zeros((1, mid_ref.shape[2]), F32) for _ in range(4)]
+    for p in range(2):
+        unit, inverse = ln_stats(mid_ref[p])
+        g = g_ref[p].astype(F32)
+        da = gather.result(p)
+        dm = g + ln_back(unit, inverse, gain_ref[...], da)
+        dm_ref[p] = dm
+        low = dm.astype(BF16)
+        db_ref[p, t] = low
+        share.push(p, p)
+        for k, term in enumerate((da * unit, da, low.astype(F32), g)):
+            rows[k] = rows[k] + jnp.sum(term, 0, keepdims=True)
+    for k in range(4):
+        sums_ref[k : k + 1, :] = rows[k]
+    collect.forward()
+    for p in range(2):
+        share.forward(p, p)
+    for p in range(2):
+        gather.finish(p)
+        share.finish(p)
+    collect.finish(wg_ref)
 
 
 def bwd_kernel(
-    heads, hd, cols, rows, qb,
-    qa_ref, ka_ref, v_ref, do_ref, o_ref, lse_ref, tab_ref, hot_ref,
-    dq_ref, dk_ref, dv_ref, rg_ref, kt_ref, acc_k, acc_v, del_ref,
+    shards, heads, hd, cols, rows, qb,
+    qa_ref, ka_ref, qkv_ref, do_ref, o_ref, lse_ref, tab_ref, hot_ref, part_ref, mid_ref, fb_ref, w_ref,
+    dqkv_ref, rg_ref, out_ref, wg_ref,
+    kt_ref, acc_k, acc_v, del_ref, res_ref, mate, far, outb, sum_sems, swap_sems, w_cross, w_line, w_sems,
 ):
-    tok = v_ref.shape[0]
+    _, me, _ = place()
+    greet(shards)
+    gather = Gather2(part_ref, mate, far, outb, sum_sems)
+    gather.push(0)
+    gather.push(1)
+    collect = Collect(shards, w_ref, w_cross, w_line, w_sems)
+    gather.forward(0)
+    gather.forward(1)
+    tok = qkv_ref.shape[0]
     scale = hd**-0.5
     c = scale * math.log2(math.e)
     rg_ref[...] = jnp.zeros_like(rg_ref)
     for h in range(heads):
         sl = slice(h * hd, (h + 1) * hd)
+        k_sl, v_sl = (slice((j * heads + h) * hd, (j * heads + h + 1) * hd) for j in (1, 2))
         pad = jnp.zeros((tok, 128 - hd), BF16)
-        vp = jnp.concatenate([v_ref[:, sl], pad], 1)
+        vp = jnp.concatenate([qkv_ref[:, v_sl], pad], 1)
         kt_ref[0:128, :] = jnp.where(lane_ids((tok, 128)) < hd, ka_ref[h, :, 0:128], hot_ref[:, 0:128]).T
         kt_ref[128:256, :] = hot_ref[:, 128:256].T
         prod = jnp.concatenate([do_ref[:, sl].astype(F32) * o_ref[:, sl], pad.astype(F32)], 1)
@@ -496,29 +811,74 @@
             d = jnp.concatenate(parts, 0).astype(BF16)
             rel = mm(d, tab_ref[...])
             rg_ref[...] += mm(d, qblk[:, 0:128], TN)
-            dq_ref[at, sl] = (scale * dqa[:, 0:128] + rel)[:, 0:hd].astype(BF16)
+            dqkv_ref[at, sl] = (scale * dqa[:, 0:128] + rel)[:, 0:hd].astype(BF16)
             return 0
 
         lax.fori_loop(0, tok // qb, blk, 0)
-        dk_ref[:, sl] = (scale * acc_k[...])[:, 0:hd].astype(BF16)
-        dv_ref[:, sl] = acc_v[...][:, 0:hd].astype(BF16)
-
-
-def attn_bwd(qa, ka, v, do, o, lse, tab, hot, heads, hd, cols, rows, qb=256):
-    tok = v.shape[0]
-    S = jax.ShapeDtypeStruct
-    return pl.pallas_call(
-        partial(bwd_kernel, heads, hd, cols, rows, qb),
-        out_shape=(S((tok, heads * hd), BF16),) * 3 + (S((256, 128), F32),),
-        scratch_shapes=[
-            pltpu.VMEM((256, tok), BF16),
-            pltpu.VMEM((tok, 128), F32),
-            pltpu.VMEM((tok, 128), F32),
-            pltpu.VMEM((8, tok), F32),
-        ],
-        compiler_params=pltpu.CompilerParams(vmem_limit_bytes=VMEM_GRANT),
-        name="attn_bwd",
-    )(qa, ka, v, do, o, lse, tab, hot)
+        dqkv_ref[:, k_sl] = (scale * acc_k[...])[:, 0:hd].astype(BF16)
+        dqkv_ref[:, v_sl] = acc_v[...][:, 0:hd].astype(BF16)
+        if h == min(1, heads - 1):
+            collect.forward()
+        if h == min(2, heads - 1):
+            for p in range(2):
+                total = mid_ref[p] + gather.result(p) + fb_ref[...]
+                res_ref[p] = total.astype(BF16)
+            swap = send(res_ref.at[1 - me], out_ref.at[me], swap_sems, 0, {"ctx": 1 - me})
+            out_ref[me] = res_ref[me]
+    for p in range(2):
+        gather.finish(p)
+    collect.finish(wg_ref)
+    swap.wait()
+
+
+def end_kernel(
+    shards, part_ref, x_ref, dm_ref, gain_ref, w_ref, small_ref, out_ref, wg_ref, total_ref,
+    res_ref, mate, far, outb, sum_sems, swap_sems, held, got, line, small_sems, w_cross, w_line, w_sems,
+):
+    s, me, t = place()
+    greet(shards)
+    gather = Gather2(part_ref, mate, far, outb, sum_sems)
+    gather.push(0)
+    gather.push(1)
+    collect = Collect(shards, w_ref, w_cross, w_line, w_sems)
+    gather.forward(0)
+    gather.forward(1)
+    first = jnp.zeros((1, x_ref.shape[2]), F32)
+    second = jnp.zeros((1, x_ref.shape[2]), F32)
+    for p in range(2):
+        unit, inverse = ln_stats(x_ref[p].astype(F32))
+        da = gather.result(p)
+        res_ref[p] = (dm_ref[p] + ln_back(unit, inverse, gain_ref[...], da)).astype(BF16)
+        first = first + jnp.sum(da * unit, 0, keepdims=True)
+        second = second + jnp.sum(da, 0, keepdims=True)
+    swap = send(res_ref.at[1 - me], out_ref.at[me], swap_sems, 0, {"ctx": 1 - me})
+    out_ref[me] = res_ref[me]
+    held[0] = small_ref[...]
+    held[0, 0:1, :] = first
+    held[0, 1:2, :] = second
+    waits = []
+    for k, peer in enumerate(({"tp": core_mate(t)}, {"tp": far_mate(t)}, {"ctx": 1 - me})):
+        copy = send(held.at[k], got.at[k], small_sems, k, peer)
+        copy.wait_recv()
+        waits.append(copy)
+        held[k + 1] = held[k] + got[k]
+    line[s] = held[3]
+    for d in range(1, shards):
+        waits.append(send(held.at[3], line.at[s], small_sems, 2 + d, {"shard": lax.rem(s + d, shards)}))
+    collect.forward()
+    for k, copy in enumerate(waits):
+        if k < 3:
+            copy.wait_send()
+        else:
+            copy.wait()
+    acc = line[0]
+    for k in range(1, shards):
+        acc = acc + line[k]
+    total_ref[...] = acc
+    for p in range(2):
+        gather.finish(p)
+    collect.finish(wg_ref)
+    swap.wait()
 
 
 def position_tables(rel_rows, rel_cols, hd):
@@ -540,33 +900,12 @@
     return first.astype(BF16), second.astype(BF16)
 
 
-def swap_halves(block):
-    mine = lax.axis_index("ctx")
-    keep = lax.dynamic_index_in_dim(block, mine, 0, keepdims=False)
-    give = lax.dynamic_index_in_dim(block, 1 - mine, 0, keepdims=False)
-    got = lax.ppermute(give, "ctx", [(0, 1), (1, 0)])
-    first = mine == 0
-    return jnp.stack([jnp.where(first, keep, got), jnp.where(first, got, keep)])
-
-
-def ln_stats(values):
-    average = jnp.mean(values, -1, keepdims=True)
-    centred = values - average
-    inverse = lax.rsqrt(jnp.mean(centred * centred, -1, keepdims=True) + EPSILON)
-    return centred * inverse, inverse
-
-
-def ln_back(unit, inverse, gain, grad):
-    scaled = grad * gain
-    first = jnp.mean(scaled, -1, keepdims=True)
-    second = jnp.mean(scaled * unit, -1, keepdims=True)
-    return inverse * (scaled - first - unit * second)
-
-
 def on_device_images(
     tokens, norm1_gain, norm1_bias, qkv_weight, qv_bias, rel_rows, rel_cols, proj_weight, proj_bias,
     norm2_gain, norm2_bias, fc1_weight, fc1_bias, fc2_weight, fc2_bias, cotangent,
 ):
+    S = jax.ShapeDtypeStruct
+    shards = lax.axis_size("shard")
     tp_count = lax.axis_size("tp")
     tp_rank = lax.axis_index("tp")
     heads = H // tp_count
@@ -574,98 +913,136 @@
     ff = FF // tp_count
     rows = (rel_rows.shape[0] + 1) // 2
     tok = rows * COLS
-    cotangent_own = swap_halves(cotangent)
-    tokens_own = swap_halves(tokens)
-    qkv_full = lax.all_gather(qkv_weight, ("shard", "ctx"), axis=1, tiled=True)
-    proj_full = lax.all_gather(proj_weight, ("shard", "ctx"), axis=1, tiled=True)
-    fc1_full = lax.all_gather(fc1_weight, ("shard", "ctx"), axis=0, tiled=True)
-    fc2_full = lax.all_gather(fc2_weight, ("shard", "ctx"), axis=1, tiled=True)
+    own = tokens.shape
+    piece = own[1:]
+    full = (2, tp_count) + piece
+    block = fc1_weight.shape
+    blocks = (2 * shards,) + block
+    qkv_cols = 3 * width
+    w1 = jnp.concatenate([qkv_weight[0], qkv_weight[1], qkv_weight[2], proj_weight.T], 1)
+    fc2_t = fc2_weight.T
     qv_local = lax.dynamic_slice_in_dim(qv_bias, tp_rank * width, width, 1)
+    qkv_bias = jnp.concatenate([qv_local[0], jnp.zeros((width,), F32), qv_local[1]])
     fc1_local = lax.dynamic_slice_in_dim(fc1_bias, tp_rank * ff, ff, 0)
-    x = tokens_own.astype(F32)
-    g = cotangent_own.astype(F32)
-
-    def gather(block):
-        return lax.all_gather(block, "tp", axis=1, tiled=True).reshape(tok, D)
-
-    def scatter(part):
-        whole = part.astype(BF16).reshape(2, tok // 2, D)
-        return lax.psum_scatter(whole, "tp", scatter_dimension=1, tiled=True).astype(F32)
-
-    unit1, inv1 = ln_stats(x)
-    a1 = gather((unit1 * norm1_gain + norm1_bias).astype(BF16))
-    q = (mm(a1, qkv_full[0]) + qv_local[0]).astype(BF16)
-    k = mm(a1, qkv_full[1]).astype(BF16)
-    v = (mm(a1, qkv_full[2]) + qv_local[1]).astype(BF16)
     tab_f, tab_b = position_tables(rel_rows, rel_cols, HD)
     hot_f, hot_b = position_hots(tok, HD, COLS, rows)
-    o, o_low, lse, qa, ka = attn_fwd(q, k, v, tab_f, hot_f, heads, HD, COLS, rows)
-    mid = x + scatter(mm(o_low, proj_full)) + proj_bias
-    unit2, inv2 = ln_stats(mid)
-    a2 = gather((unit2 * norm2_gain + norm2_bias).astype(BF16))
-    cot = gather(cotangent_own)
+    spread = Spread.scratch(shards)
+    collect = Collect.scratch(shards, block)
+    gather = Gather2.scratch(piece)
+    swap = [DMA((2, 1))]
+    share = [DMA((2, 6))]
+
+    def row(vec):
+        return vec.reshape(1, -1)
+
+    x, a1, w1_full = comm_call(
+        partial(front_kernel, shards), "front", 0,
+        (tokens, w1, row(norm1_gain), row(norm1_bias)),
+        (S(own, BF16), S(full, BF16), S(blocks, BF16)),
+        swap + share + spread, hbm_in=(1,), hbm_out=(2,),
+    )
+    a1 = a1.reshape(tok, D)
+    w1_full = w1_full.reshape(D, -1)
+    qkv_full = w1_full[:, :qkv_cols]
+    proj_full = w1_full[:, qkv_cols:]
+    qkv = (mm(a1, qkv_full) + qkv_bias).astype(BF16)
+    o, o_low, lse, qa, ka, g, cot, fc1_full = comm_call(
+        partial(fwd_kernel, shards, heads, HD, COLS, rows, 256), "attn_fwd", 1,
+        (qkv, tab_f, hot_f, cotangent, fc1_weight),
+        (
+            S((tok, width), F32), S((tok, width), BF16), S((heads, tok), F32),
+            S((heads, tok, 256), BF16), S((heads, tok, 256), BF16),
+            S(own, BF16), S(full, BF16), S(blocks, BF16),
+        ),
+        swap + share + spread, hbm_in=(4,), hbm_out=(7,),
+    )
+    fc1_full = fc1_full.reshape(D, ff)
+    cot = cot.reshape(tok, D)
+    proj_part = mm(o_low, proj_full, NT).astype(BF16).reshape(full)
+    mid, a2, fc2_full = comm_call(
+        partial(mid_kernel, shards), "mid", 2,
+        (proj_part, x, row(proj_bias), row(norm2_gain), row(norm2_bias), fc2_t),
+        (S(own, F32), S(full, BF16), S(blocks, BF16)),
+        gather + share + spread, hbm_in=(5,), hbm_out=(2,),
+    )
+    a2 = a2.reshape(tok, D)
+    fc2_full = fc2_full.reshape(D, ff)
     pre = mm(a2, fc1_full) + fc1_local
     cdf = 0.5 * (1.0 + lax.erf(pre * (2.0**-0.5)))
     act = (pre * cdf).astype(BF16)
     slope = cdf + pre * jnp.exp(-0.5 * pre * pre) * ((2.0 * math.pi) ** -0.5)
-    d_pre = (mm(cot, fc2_full, NT) * slope).astype(BF16)
-    d_a2 = scatter(mm(d_pre, fc1_full, NT))
-    output = (mid + scatter(mm(act, fc2_full)) + fc2_bias).astype(BF16)
-    fc2_grad = mm(act, cot, TN)
-    fc1_grad = mm(a2, d_pre, TN)
-    d_mid = g + ln_back(unit2, inv2, norm2_gain, d_a2)
-    d_branch = d_mid.astype(BF16)
-    d_branch_full = gather(d_branch)
-    d_o = mm(d_branch_full, proj_full, NT).astype(BF16)
-    proj_grad = mm(o_low, d_branch_full, TN)
-    dq, dk, dv, rel_grad = attn_bwd(qa, ka, v, d_o, o, lse, tab_b, hot_b, heads, HD, COLS, rows)
-    d_a1 = scatter(mm(dq, qkv_full[0], NT) + mm(dk, qkv_full[1], NT) + mm(dv, qkv_full[2], NT))
-    qkv_grad = jnp.stack([mm(a1, dq, TN), mm(a1, dk, TN), mm(a1, dv, TN)])
-    tokens_grad = (d_mid + ln_back(unit1, inv1, norm1_gain, d_a1)).astype(BF16)
-
-    def reduce(part, dim):
-        return lax.psum_scatter(
-            part.astype(BF16), ("shard", "ctx"), scatter_dimension=dim, tiled=True
-        ).astype(F32)
-
-    def total(part):
-        return jnp.sum(part.astype(F32), tuple(range(part.ndim - 1)))
-
-    qv_part = jnp.stack([total(dq), total(dv)])
+    d_pre = (mm(cot, fc2_full) * slope).astype(BF16)
+    d_a2 = mm(d_pre, fc1_full, NT).astype(BF16).reshape(full)
+    fc2_grad = mm(cot, act, TN).astype(BF16).reshape(blocks)
+    d_mid, d_branch, fc2_own, sums = comm_call(
+        partial(turn_kernel, shards), "turn", 3,
+        (d_a2, mid, g, row(norm2_gain), fc2_grad),
+        (S(own, F32), S(full, BF16), S(block, F32), S((4, D), F32)),
+        gather + share + collect,
+    )
+    fc1_grad = mm(a2, d_pre, TN).astype(BF16).reshape(blocks)
+    mlp_part = mm(act, fc2_full, NT).astype(BF16).reshape(full)
+    d_branch = d_branch.reshape(tok, D)
+    d_o = mm(d_branch, proj_full).astype(BF16)
+    dqkv, rel_grad, output, fc1_own = comm_call(
+        partial(bwd_kernel, shards, heads, HD, COLS, rows, 256), "attn_bwd", 4,
+        (qa, ka, qkv, d_o, o, lse, tab_b, hot_b, mlp_part, mid, row(fc2_bias), fc1_grad),
+        (S((tok, qkv_cols), BF16), S((256, 128), F32), S(own, BF16), S(block, F32)),
+        [
+            pltpu.VMEM((256, tok), BF16), pltpu.VMEM((tok, 128), F32), pltpu.VMEM((tok, 128), F32),
+            pltpu.VMEM((8, tok), F32), pltpu.VMEM(own, BF16),
+        ] + gather + swap + collect,
+    )
+    d_a1 = mm(dqkv, qkv_full, NT).astype(BF16).reshape(full)
+    w1_grad = jnp.concatenate([mm(a1, dqkv, TN), mm(d_branch, o_low, TN)], 1).astype(BF16).reshape(blocks)
+    qkv_sum = jnp.sum(dqkv.astype(F32), 0)
+    qv_part = jnp.stack([qkv_sum[:width], qkv_sum[2 * width :]])
     qv_placed = lax.dynamic_update_slice_in_dim(jnp.zeros((2, D), F32), qv_part, tp_rank * width, 1)
-    fc1_placed = lax.dynamic_update_slice_in_dim(jnp.zeros((FF,), F32), total(d_pre), tp_rank * ff, 0)
-    small = lax.psum(
-        (
-            total(d_a1 * unit1),
-            total(d_a1),
-            qv_placed,
-            rel_grad[: rel_rows.shape[0], :HD],
-            rel_grad[128 : 128 + rel_cols.shape[0], :HD],
-            total(d_branch),
-            total(d_a2 * unit2),
-            total(d_a2),
-            fc1_placed,
-            total(cotangent),
-        ),
-        ("shard", "ctx", "tp"),
-    )
+    fc1_sum = jnp.sum(d_pre.astype(F32), 0)
+    fc1_placed = lax.dynamic_update_slice_in_dim(jnp.zeros((FF,), F32), fc1_sum, tp_rank * ff, 0)
+    terms = (
+        jnp.zeros((2 * D,), F32),
+        qv_placed.reshape(-1),
+        fc1_placed,
+        sums.reshape(-1),
+        rel_grad[: rel_rows.shape[0], :HD].reshape(-1),
+        rel_grad[128 : 128 + rel_cols.shape[0], :HD].reshape(-1),
+    )
+    count = sum(term.shape[0] for term in terms)
+    lines = -(-count // (8 * D)) * 8
+    packed = jnp.concatenate(terms + (jnp.zeros((lines * D - count,), F32),)).reshape(lines, D)
+    tokens_grad, w1_own, total = comm_call(
+        partial(end_kernel, shards), "end", 5,
+        (d_a1, x, d_mid, row(norm1_gain), w1_grad, packed),
+        (S(own, BF16), S(block, F32), S((lines, D), F32)),
+        [pltpu.VMEM(own, BF16)] + gather + swap
+        + [
+            pltpu.VMEM((4, lines, D), F32), pltpu.VMEM((3, lines, D), F32),
+            pltpu.VMEM((shards, lines, D), F32), DMA((2, 2 + shards)),
+        ]
+        + collect,
+    )
+    flat = total.reshape(-1)
+    base = 4 * D + FF
+    rel_at = base + 4 * D
+    rel_mid = rel_at + rel_rows.size
     return (
-        swap_halves(output),
-        swap_halves(tokens_grad),
-        small[0],
-        small[1],
-        reduce(qkv_grad, 1),
-        small[2],
-        small[3],
-        small[4],
-        reduce(proj_grad, 1),
-        small[5],
-        small[6],
-        small[7],
-        reduce(fc1_grad, 0),
-        small[8],
-        reduce(fc2_grad, 1),
-        small[9],
+        output,
+        tokens_grad,
+        total[0],
+        total[1],
+        jnp.stack([w1_own[:, j * width : (j + 1) * width] for j in range(3)]),
+        total[2:4],
+        flat[rel_at:rel_mid].reshape(rel_rows.shape),
+        flat[rel_mid : rel_mid + rel_cols.size].reshape(rel_cols.shape),
+        w1_own[:, qkv_cols:].T,
+        flat[base + 2 * D : base + 3 * D],
+        flat[base : base + D],
+        flat[base + D : base + 2 * D],
+        fc1_own,
+        flat[4 * D : base],
+        fc2_own.T,
+        flat[base + 3 * D : base + 4 * D],
     )
 
 

time: 1020 us -> 510 us (0.50)
  waiting for transfers between devices: 746 us -> 0 us
  Pallas kernels: 57.7 us -> 404 us
  blocking collectives: 30.7 us -> 0 us
  other arithmetic: 36.5 us -> 9.59 us
  matrix products: 82.7 us -> 61.4 us
  between operations: 14.6 us -> 1.26 us
    pallas_call x2 -> x6, Pallas kernels: 57.7 us -> 404 us  [comm_call(): pl.pallas_call(kernel, out_shape=tuple(outs), in_specs=[ANY if i in hbm_i...]
    reduce_scatter x7 -> x0, waiting for transfers between devices: 280 us -> none  [the longest x3 187 us: reduce(): lax.psum_scatter(part.astype(BF16), ('shard', 'ctx'), scatter_dimension=d...]
    all_gather x7 -> x0, waiting for transfers between devices: 230 us -> none  [the longest x4 69.7 us: gather(): return lax.all_gather(block, 'tp', axis=1, tiled=True).reshape(tok, D)]
    psum x1 -> x0, waiting for transfers between devices: 136 us -> none  [on_device_images(): lax.psum((total(d_a1 * unit1), total(d_a1), qv_placed, rel_grad[:rel_rows...]
    unnamed x17 -> x0, waiting for transfers between devices: 73.4 us -> none
    all_gather x1 -> x0, blocking collectives: 30.7 us -> none  [on_device_images(): lax.all_gather(proj_weight, ('shard', 'ctx'), axis=1, tiled=True)]
    ppermute x4 -> x0, waiting for transfers between devices: 26.5 us -> none  [swap_halves(): got = lax.ppermute(give, 'ctx', [(0, 1), (1, 0)])]
    dot_general x18 -> x12, matrix products: 82.7 us -> 61.4 us  [mm(): return lax.dot_general(left, right, dims, preferred_element_type=F32)]
  transfers between devices with their start and end apart: 20 -> 0, of which waited for: 17 -> 0; matrix products, arithmetic and copies ran while one was open for 10% -> 0% of each run, Pallas kernels for 0% -> 0%
where the time goes in v2:
time: 510 us; the launch traced here: 506 us
  Pallas kernels  404 us (79%)
  matrix products  61.4 us (12%)
  local copies, waits for them, and re-layouts  30.3 us (6%)
  other arithmetic  9.59 us (2%)
    pallas_call x6, Pallas kernels, comm_call(): pl.pallas_call(kernel, out_shape=tuple(outs), in_specs=[ANY if i in hbm_i...  404 us
    dot_general x12, matrix products, mm(): return lax.dot_general(left, right, dims, preferred_element_type=F32)  61.4 us

profile of v2, /device:TPU:8, one launch (start us, length us, event | category | flops | bytes accessed | tf_op | source)
XLA Modules:
  0.0 506.1 jit_solution(2163862469538059120)
XLA Ops:
  7.1 52.6 %front.1 = (bf16[2,128,1280]{2,1,0:T(8,128)(2,1)}, bf16[2,4,128,1280]{3,2,1,0:T(8,128)(2,1)}, bf16[8,160,1280]{2,1,0:T(8,128)(2,1)}) custom-call(bf16[2,128,1280]{2,1,0:T(8,128)(2,1)} %tok_ref.1, bf16[160,1280]{1,0:T(8,128)(2,1)} %concatenate.20.w_ref, f32[1,1280]{1,0:T(1,128)} %reshape.125.gain_ref, f32[1,1280]{1,0:T(1,128)} %reshape.126.bias_ref), custom_call_target="tpu_custom_call" | custom-call | tf_op jit(solution)/shard_map/front/pallas_call | solution.py:584
  59.8 6.8 %add_convert_fusion.qkv_ref = bf16[1024,960]{1,0:T(8,128)(2,1)} fusion(f32[960]{0:T(1024)S(1)} %pad_maximum_fusion.2, bf16[1024,1280]{1,0:T(8,128)(2,1)} %bitcast.67, bf16[1280,1280]{1,0:T(8,128)(2,1)} %bitcast.79), kind=kOutput, calls=%fused_computation.13 | convolution fusion | flops 2518548480 | bytes 7212800 | tf_op jit(solution)/shard_map/dot_general | solution.py:388
  66.6 2.7 fusion.17
  70.2 65.2 %attn_fwd.1 = (f32[1024,320]{1,0:T(8,128)}, bf16[1024,320]{1,0:T(8,128)(2,1)}, f32[4,1024]{1,0:T(4,128)}, bf16[4,1024,256]{2,1,0:T(8,128)(2,1)}, bf16[4,1024,256...) custom-call(bf16[1024,960]{1,0:T(8,128)(2,1)} %add_convert_fusion.qk, ...), custom_call_target="tpu_custom_call" | custom-call | tf_op jit(solution)/shard_map/attn_fwd/pallas_call | solution.py:584
  135.4 4.7 convolution_convert_fusion.2
  141.9 55.7 %mid.1 = (f32[2,128,1280]{2,1,0:T(8,128)}, bf16[2,4,128,1280]{3,2,1,0:T(8,128)(2,1)}, bf16[8,160,1280]{2,1,0:T(8,128)(2,1)}) custom-call(bf16[2,4,128,1280]{3,2,1,0:T(8,128)(2,1)} %bitcast.72, bf16[2,128,1280]{2,1,0:T(8,128)(2,1)} %get-tuple-element.47.x_ref, f32[1,1280]{1,0:T(1,128)} %reshape.131.pb_ref, f32[1,1280]{1,0:T(1,128)} %reshape.132.gain_ref, ...), custom_call_target="tpu_custom_call" | custom-call | tf_op jit(solution)/shard_map/mid/pallas_call | solution.py:584
  198.4 5.7 %multiply_convert_fusion = (bf16[1024,1280]{1,0:T(8,128)(2,1)S(1)}, f32[1024,1280]{1,0:T(8,128)S(1)}) fusion(f32[1280]{0:T(1024)S(1)} %dynamic_slice.7, bf16[1024,1280]{1,0:T(8,128)(2,1)} %bitcast.89, bf16[1280,1280]{1,0:T(8,128)(2,1)S(1)} %bitcast.83), kind=kOutput, calls=%fused_computation.10 | convolution fusion | flops 3363307520 | bytes 13767680 | tf_op jit(solution)/shard_map/dot_general | solution.py:388
  204.1 5.9 %convert_reduce_fusion = (f32[1280]{0:T(1024)S(1)}, bf16[1024,1280]{1,0:T(8,128)(2,1)S(1)}) fusion(f32[1024,1280]{1,0:T(8,128)S(1)} %get-tuple-element.118, f32[1280]{0:T(1024)S(1)} %dynamic_slice.7, bf16[1024,1280]{1,0:T(8,128)(2,1)S(1)} %bitcast.87, bf16[1280,1280]{1,0:T(8,128)(2,1)S(1)} %bitcast.85), kind=kOutput, calls=%fused_computation.9 | convolution fusion | flops 3372481280 | bytes 13772800 | tf_op jit(solution)/shard_map/dot_general | solution.py:388
  210.0 5.1 %convolution_convert_fusion = bf16[1280,1280]{1,0:T(8,128)(2,1)} fusion(bf16[1024,1280]{1,0:T(8,128)(2,1)S(1)} %bitcast.90, bf16[1024,1280]{1,0:T(8,128)(2,1)S(1)} %get-tuple-element.120), kind=kOutput, calls=%fused_computation.1 | convolution fusion | flops 3357081600 | bytes 8519680 | tf_op jit(solution)/shard_map/dot_general | solution.py:388
  215.1 4.9 convolution_convert_fusion.3
  219.9 5.1 %convolution_convert_fusion.1 = bf16[1280,1280]{1,0:T(8,128)(2,1)} fusion(bf16[1024,1280]{1,0:T(8,128)(2,1)S(1)} %bitcast.88, bf16[1024,1280]{1,0:T(8,128)(2,1)S(1)} %get-tuple-element.117), kind=kOutput, calls=%fused_computation.2 | convolution fusion | flops 3357081600 | bytes 8519680 | tf_op jit(solution)/shard_map/dot_general | solution.py:388
  225.1 5.2 %convolution_convert_fusion.4 = bf16[1024,1280]{1,0:T(8,128)(2,1)} fusion(bf16[1024,1280]{1,0:T(8,128)(2,1)S(1)} %get-tuple-element.120, bf16[1280,1280]{1,0:T(8,128)(2,1)S(1)} %bitcast.84), kind=kOutput, calls=%fused_computation.16 | convolution fusion | flops 3356753920 | bytes 8519680 | tf_op jit(solution)/shard_map/dot_general | solution.py:388
  230.3 67.8 %turn.1 = (f32[2,128,1280]{2,1,0:T(8,128)}, bf16[2,4,128,1280]{3,2,1,0:T(8,128)(2,1)}, f32[160,1280]{1,0:T(8,128)}, f32[4,1280]{1,0:T(4,128)}) custom-call(bf16[2,4,128,1280]{3,2,1,0:T(8,128)(2,1)} %bitcast.75, f32[2,128,1280]{2,1,0:T(8,128)} %get-tuple-element.51.mid_ref, bf16[2,128,1280]{2,1,0:T(8,128)(2,1)} %get-tuple-element.52.g_ref, ...), custom_call_target="tpu_custom_call" | custom-call | tf_op jit(solution)/shard_map/turn/pallas_call | solution.py:584
  298.1 3.4 convolution_convert_fusion.7
  304.0 63.2 %attn_bwd.1 = (bf16[1024,960]{1,0:T(8,128)(2,1)}, f32[256,128]{1,0:T(8,128)}, bf16[2,128,1280]{2,1,0:T(8,128)(2,1)}, f32[160,1280]{1,0:T(8,128)}) custom-call(bf16[4,1024,256]{2,1,0:T(8,128)(2,1)} %get-tuple-element.43.qa_ref, bf16[4,1024,256]{2,1,0:T(8,128)(2,1)} %get-tuple-element.44.ka_ref, bf16[1024,960]{1,0:T(8,128)(2,1)} %add_convert_fusion.qkv_ref, ...), custom_call_target="tpu_custom_call" | custom-call | tf_op jit(solution)/shard_map/attn_bwd/pallas_call | solution.py:584
  367.2 2.1 convert_reduce_fusion.1
  372.5 2.8 copy.54
  375.3 6.9 %fusion.11 = bf16[8,160,960]{2,1,0:T(8,128)(2,1)} fusion(bf16[8,160,1024]{2,1,0:T(8,128)(2,1)} %bitcast.74, bf16[1024,960]{1,0:T(8,128)(2,1)} %get-tuple-element.57), kind=kOutput, calls=%fused_computation.28 | convolution fusion | flops 2517811200 | bytes 7045120 | tf_op jit(solution)/shard_map/dot_general | solution.py:388
  382.2 2.8 copy.56
  385.0 3.4 convolution_convert_fusion.6
  388.5 2.5 pad_maximum_fusion.w_ref
  392.2 4.5 convolution_convert_fusion.5
  396.7 99.1 %end.1 = (bf16[2,128,1280]{2,1,0:T(8,128)(2,1)}, f32[160,1280]{1,0:T(8,128)}, f32[24,1280]{1,0:T(8,128)}) custom-call(bf16[2,4,128,1280]{3,2,1,0:T(8,128)(2,1)} %bitcast.71, bf16[2,128,1280]{2,1,0:T(8,128)(2,1)} %get-tuple-element.47.x_ref, f32[2,128,1280]{2,1,0:T(8,128)} %get-tuple-element.58.dm_ref, f32[1,1280]{1,0:T(1,128)} %reshape.125.gain_ref, ...), custom_call_target="tpu_custom_call" | custom-call | tf_op jit(solution)/shard_map/end/pallas_call | solution.py:584
  495.8 2.3 slice_bitcast_fusion
  (97 shorter events, 24.6 us)
Async XLA Ops:
  59.8 9.5 %copy-start.10 = (bf16[31,80]{1,0:T(8,128)(2,1)S(1)}, bf16[31,80]{1,0:T(8,128)(2,1)}, u32[]{:S(2)}) copy-start(bf16[31,80]{1,0:T(8,128)(2,1)} %param.21) | copy-start | bytes 14884
  59.8 9.7 %copy-start.9 = (bf16[127,80]{0,1:T(8,128)(2,1)S(1)}, bf16[127,80]{0,1:T(8,128)(2,1)}, u32[]{:S(2)}) copy-start(bf16[127,80]{0,1:T(8,128)(2,1)} %param.22) | copy-start | bytes 60964
  135.4 4.7 copy-start.12
  135.4 5.3 %copy-start.13 = (f32[1280]{0:T(1024)S(1)}, f32[1280]{0:T(1024)}, u32[]{:S(2)}) copy-start(f32[1280]{0:T(1024)} %param.24) | copy-start | bytes 15364
  135.4 5.9 %copy-start.14 = (f32[1280]{0:T(1024)S(1)}, f32[1280]{0:T(1024)}, u32[]{:S(2)}) copy-start(f32[1280]{0:T(1024)} %param.26) | copy-start | bytes 15364
  135.4 63.0 %copy-start.17 = (bf16[8,160,1280]{2,1,0:T(8,128)(2,1)S(1)}, bf16[8,160,1280]{2,1,0:T(8,128)(2,1)}, u32[]{:S(2)}) copy-start(bf16[8,160,1280]{2,1,0:T(8,128)(2,1)} %get-tuple-element.50) | copy-start | bytes 9830404
  198.4 5.7 %copy-start.18 = (bf16[8,160,1280]{2,1,0:T(8,128)(2,1)S(1)}, bf16[8,160,1280]{2,1,0:T(8,128)(2,1)}, u32[]{:S(2)}) copy-start(bf16[8,160,1280]{2,1,0:T(8,128)(2,1)} %get-tuple-element.48) | copy-start | bytes 9830404
  198.4 5.7 %copy-start.19 = (bf16[2,4,128,1280]{3,2,1,0:T(8,128)(2,1)S(1)}, bf16[2,4,128,1280]{3,2,1,0:T(8,128)(2,1)}, u32[]{:S(2)}) copy-start(bf16[2,4,128,1280]{3,2,1,0:T(8,128)(2,1)} %get-tuple-element.45) | copy-start | bytes 7864324
  204.1 5.9 %copy-start.20 = (bf16[2,4,128,1280]{3,2,1,0:T(8,128)(2,1)S(1)}, bf16[2,4,128,1280]{3,2,1,0:T(8,128)(2,1)}, u32[]{:S(2)}) copy-start(bf16[2,4,128,1280]{3,2,1,0:T(8,128)(2,1)} %get-tuple-element.49) | copy-start | bytes 7864324
  298.1 5.4 %copy-start.15 = (f32[1280]{0:T(1024)S(1)}, f32[1280]{0:T(1024)}, u32[]{:S(2)}) copy-start(f32[1280]{0:T(1024)} %param.30) | copy-start | bytes 15364
  304.0 67.3 %copy-start.11 = (f32[4,1280]{1,0:T(4,128)S(1)}, f32[4,1280]{1,0:T(4,128)}, u32[]{:S(2)}) copy-start(f32[4,1280]{1,0:T(4,128)} %get-tuple-element.59) | copy-start | bytes 61444
  367.2 5.3 %copy-start = (bf16[2,4,128,1280]{3,2,1,0:T(8,128)(2,1)S(1)}, bf16[2,4,128,1280]{3,2,1,0:T(8,128)(2,1)}, u32[]{:S(2)}) copy-start(bf16[2,4,128,1280]{3,2,1,0:T(8,128)(2,1)} %get-tuple-element.41) | copy-start | bytes 7864324
  375.3 6.9 %copy-start.1 = (bf16[2,4,128,1280]{3,2,1,0:T(8,128)(2,1)S(1)}, bf16[2,4,128,1280]{3,2,1,0:T(8,128)(2,1)}, u32[]{:S(2)}) copy-start(bf16[2,4,128,1280]{3,2,1,0:T(8,128)(2,1)} %get-tuple-element.53) | copy-start | bytes 7864324
  382.2 2.8 copy-start.21
  385.0 3.4 copy-start.2
  388.5 2.5 copy-start.3
  388.5 3.7 copy-start.16
  495.7 3.3 copy-start.8
  495.8 6.6 %copy-start.6 = (bf16[2,128,1280]{2,1,0:T(8,128)(2,1)S(1)}, bf16[2,128,1280]{2,1,0:T(8,128)(2,1)}, u32[]{:S(2)}) copy-start(bf16[2,128,1280]{2,1,0:T(8,128)(2,1)} %get-tuple-element.143) | copy-start | bytes 1966084
  495.8 7.5 %copy-start.7 = (bf16[2,128,1280]{2,1,0:T(8,128)(2,1)S(1)}, bf16[2,128,1280]{2,1,0:T(8,128)(2,1)}, u32[]{:S(2)}) copy-start(bf16[2,128,1280]{2,1,0:T(8,128)(2,1)} %get-tuple-element.144) | copy-start | bytes 1966084
  495.8 8.3 %copy-start.5 = (f32[160,1280]{1,0:T(8,128)S(1)}, f32[160,1280]{1,0:T(8,128)}, u32[]{:S(2)}) copy-start(f32[160,1280]{1,0:T(8,128)} %get-tuple-element.155) | copy-start | bytes 2457604
  498.1 6.9 %copy-start.4 = (f32[160,1280]{1,0:T(8,128)S(1)}, f32[160,1280]{1,0:T(8,128)}, u32[]{:S(2)}) copy-start(f32[160,1280]{1,0:T(8,128)} %get-tuple-element.65) | copy-start | bytes 2457604

commit v3 on v2

--- a/solution.py
+++ b/solution.py
@@ -427,75 +427,111 @@
     pl.semaphore_wait(barrier, len(peers))
 
 
+def pieces_of(rows):
+    return 5 if rows % 80 == 0 else 1
+
+
 class Spread:
     def __init__(self, shards, src, dst, sems, local):
         s, c, _ = place()
         self.shards, self.dst, self.sems = shards, dst, sems
+        self.pieces = pieces_of(src.shape[0])
+        self.rows = src.shape[0] // self.pieces
         own = 2 * s + c
         self.local = pltpu.make_async_copy(src, dst.at[own], local)
         self.local.start()
-        self.along = [
-            send(src, dst.at[own], sems, d, {"shard": lax.rem(s + d, shards)}) for d in range(1, shards)
-        ]
-        self.across = [send(src, dst.at[own], sems, 0, {"ctx": 1 - c})]
-
-    def forward(self):
+        self.along, self.across = {}, []
+        for k in range(self.pieces):
+            here, there = src.at[self.span(k)], dst.at[own, self.span(k)]
+            for d in range(1, shards):
+                self.along[d, k] = send(here, there, sems, self.slot(d, k), {"shard": lax.rem(s + d, shards)})
+            self.across.append(send(here, there, sems, self.slot(0, k), {"ctx": 1 - c}))
+
+    def span(self, k):
+        return pl.ds(k * self.rows, self.rows)
+
+    def slot(self, d, k):
+        return d * self.pieces + k
+
+    def step(self, k):
         s, c, _ = place()
         for d in range(1, self.shards):
-            self.along[d - 1].wait_recv()
-            block = self.dst.at[2 * lax.rem(s + self.shards - d, self.shards) + c]
-            self.across.append(send(block, block, self.sems, self.shards + d - 1, {"ctx": 1 - c}))
+            self.along[d, k].wait_recv()
+            block = self.dst.at[2 * lax.rem(s + self.shards - d, self.shards) + c, self.span(k)]
+            slot = self.slot(self.shards + d - 1, k)
+            self.across.append(send(block, block, self.sems, slot, {"ctx": 1 - c}))
 
     def finish(self):
         self.local.wait()
-        for copy in self.along:
+        for copy in self.along.values():
             copy.wait_send()
         for copy in self.across:
             copy.wait()
 
     @staticmethod
-    def scratch(shards):
-        return [DMA((2, 2 * shards - 1)), DMA]
+    def scratch(shards, block):
+        return [DMA((2, (2 * shards - 1) * pieces_of(block[0]))), DMA]
 
 
 class Collect:
     def __init__(self, shards, src, cross, line, sems):
-        s, c, _ = place()
         self.shards, self.src, self.cross, self.line, self.sems = shards, src, cross, line, sems
-        self.across = []
-        for d in range(shards):
-            to = lax.rem(s + d + 1, shards)
-            self.across.append(send(src.at[2 * to + 1 - c], cross.at[d], sems, d, {"ctx": 1 - c}))
-
-    def forward(self):
-        s, c, _ = place()
-        self.along = []
+        self.block = cross.shape[1]
+        self.pieces = pieces_of(self.block)
+        self.rows = self.block // self.pieces
+        self.across, self.along = {}, {}
+        for k in range(min(2, self.pieces)):
+            self.push(k)
+
+    def span(self, k):
+        return pl.ds(k * self.rows, self.rows)
+
+    def part(self, owner, k):
+        return pl.ds(pl.multiple_of(owner * self.block + k * self.rows, self.rows), self.rows)
+
+    def target(self, d):
+        s, _, _ = place()
+        return lax.rem(s + d + 1, self.shards)
+
+    def push(self, k):
+        _, c, _ = place()
         for d in range(self.shards):
-            to = lax.rem(s + d + 1, self.shards)
-            self.across[d].wait_recv()
+            there = self.src.at[self.part(2 * self.target(d) + 1 - c, k)]
+            slot = d * self.pieces + k
+            self.across[d, k] = send(there, self.cross.at[d, self.span(k)], self.sems, slot, {"ctx": 1 - c})
+
+    def step(self, k):
+        _, c, _ = place()
+        if k + 2 < self.pieces:
+            self.push(k + 2)
+        at = self.span(k)
+        for d in range(self.shards):
+            self.across[d, k].wait_recv()
             if d < self.shards - 1:
-                both = self.src[2 * to + c].astype(F32) + self.cross[d].astype(F32)
-                self.cross[d] = both.astype(BF16)
-                self.along.append(
-                    send(self.cross.at[d], self.line.at[d], self.sems, self.shards + d, {"shard": to})
-                )
+                both = self.src[self.part(2 * self.target(d) + c, k)].astype(F32) + self.cross[d, at].astype(F32)
+                self.cross[d, at] = both.astype(BF16)
+                slot = (self.shards + d) * self.pieces + k
+                here, there = self.cross.at[d, at], self.line.at[d, at]
+                self.along[d, k] = send(here, there, self.sems, slot, {"shard": self.target(d)})
 
     def finish(self, out):
         s, c, _ = place()
-        for copy in self.across:
+        for copy in self.across.values():
             copy.wait_send()
-        acc = self.src[2 * s + c].astype(F32) + self.cross[self.shards - 1].astype(F32)
-        for d, copy in enumerate(self.along):
-            copy.wait()
-            acc = acc + self.line[d].astype(F32)
-        out[...] = acc
+        for k in range(self.pieces):
+            at = self.span(k)
+            acc = self.src[self.part(2 * s + c, k)].astype(F32) + self.cross[self.shards - 1, at].astype(F32)
+            for d in range(self.shards - 1):
+                self.along[d, k].wait()
+                acc = acc + self.line[d, at].astype(F32)
+            out[at] = acc
 
     @staticmethod
     def scratch(shards, block):
         return [
             pltpu.VMEM((shards,) + block, BF16),
             pltpu.VMEM((max(shards - 1, 1),) + block, BF16),
-            DMA((2, 2 * shards - 1)),
+            DMA((2, (2 * shards - 1) * pieces_of(block[0]))),
         ]
 
 
@@ -578,6 +614,24 @@
     first = jnp.mean(scaled, -1, keepdims=True)
     second = jnp.mean(scaled * unit, -1, keepdims=True)
     return inverse * (scaled - first - unit * second)
+
+
+def row_tiles(out_ref, left_ref, right_ref, dims, first, count, tile=256):
+    def one(i, _):
+        at = pl.ds(pl.multiple_of(i * tile, tile), tile)
+        out_ref[at, :] = mm(left_ref[at, :], right_ref[...], dims).astype(out_ref.dtype)
+        return 0
+
+    lax.fori_loop(first, first + count, one, 0)
+
+
+def grad_tiles(out_ref, left_ref, right_ref, first, count, cols=slice(None), tile=256):
+    def one(i, _):
+        at = pl.ds(pl.multiple_of(i * tile, tile), tile)
+        out_ref[at, cols] = mm(left_ref[:, at], right_ref[...], TN).astype(out_ref.dtype)
+        return 0
+
+    lax.fori_loop(first, first + count, one, 0)
 
 
 def comm_call(kernel, name, ident, args, outs, scratch, hbm_in=(), hbm_out=()):
@@ -614,9 +668,12 @@
     swap.wait()
     a_ref[1 - c, t] = norm(x_ref[1 - c])
     share.push(1, 1 - c)
-    share.forward(0, c)
-    spread.forward()
-    share.forward(1, 1 - c)
+    for k in range(spread.pieces):
+        spread.step(k)
+        if k == 0:
+            share.forward(0, c)
+        if k == min(2, spread.pieces - 1):
+            share.forward(1, 1 - c)
     share.finish(0)
     share.finish(1)
     spread.finish()
@@ -624,8 +681,8 @@
 
 def fwd_kernel(
     shards, heads, hd, cols, rows, qb,
-    qkv_ref, tab_ref, hot_ref, cot_ref, w_ref,
-    o_ref, ob_ref, lse_ref, qa_ref, ka_ref, g_ref, cf_ref, wf_ref,
+    qkv_ref, tab_ref, hot_ref, cot_ref, w_ref, pw_ref,
+    o_ref, ob_ref, lse_ref, qa_ref, ka_ref, g_ref, cf_ref, wf_ref, pp_ref,
     swap_sems, share_sems, w_sems, w_local,
 ):
     _, me, t = place()
@@ -681,18 +738,23 @@
             swap.wait()
             cf_ref[1 - me, t] = g_ref[1 - me]
             share.push(1, 1 - me, g_ref.at[1 - me])
+        if h < spread.pieces:
+            spread.step(h)
         if h == min(1, heads - 1):
-            spread.forward()
-        if h == heads - 1:
             share.forward(0, me)
+        if h == min(2, heads - 1):
             share.forward(1, 1 - me)
+    row_tiles(pp_ref, ob_ref, pw_ref, NT, 0, tok // 256)
+    for k in range(heads, spread.pieces):
+        spread.step(k)
     share.finish(0)
     share.finish(1)
     spread.finish()
 
 
 def mid_kernel(
-    shards, part_ref, x_ref, pb_ref, gain_ref, bias_ref, w_ref, mid_ref, a_ref, wf_ref,
+    shards, part_ref, x_ref, pb_ref, gain_ref, bias_ref, w_ref, f1_ref, fb_ref,
+    mid_ref, a_ref, wf_ref, act_ref, slope_ref,
     mate, far, outb, sum_sems, share_sems, w_sems, w_local,
 ):
     _, _, t = place()
@@ -704,23 +766,48 @@
     share = Share(a_ref, share_sems)
     gather.forward(0)
     gather.forward(1)
+    last = spread.pieces - 1
     for p in range(2):
+        if p <= last:
+            spread.step(p)
         mid = x_ref[p].astype(F32) + gather.result(p) + pb_ref[...]
         mid_ref[p] = mid
         unit, _ = ln_stats(mid)
         a_ref[p, t] = (unit * gain_ref[...] + bias_ref[...]).astype(BF16)
         share.push(p, p)
-    spread.forward()
     for p in range(2):
+        if p + 2 <= last:
+            spread.step(p + 2)
         share.forward(p, p)
+    half = a_ref.shape[1] * a_ref.shape[2]
+
+    def hidden(p):
+        def one(i, _):
+            rows = a_ref[p, pl.ds(2 * i, 2)].reshape(-1, a_ref.shape[3])
+            pre = mm(rows, f1_ref[...]) + fb_ref[...]
+            cdf = 0.5 * (1.0 + lax.erf(pre * (2.0**-0.5)))
+            bell = jnp.exp(-0.5 * pre * pre) * ((2.0 * math.pi) ** -0.5)
+            at = pl.ds(pl.multiple_of(p * half + i * rows.shape[0], 128), rows.shape[0])
+            act_ref[at, :] = (pre * cdf).astype(BF16)
+            slope_ref[at, :] = cdf + pre * bell
+            return 0
+
+        lax.fori_loop(0, a_ref.shape[1] // 2, one, 0)
+
+    share.finish(0)
+    hidden(0)
+    for k in range(4, spread.pieces):
+        spread.step(k)
+    share.finish(1)
+    hidden(1)
     for p in range(2):
         gather.finish(p)
-        share.finish(p)
     spread.finish()
 
 
 def turn_kernel(
-    shards, part_ref, mid_ref, g_ref, gain_ref, w_ref, dm_ref, db_ref, wg_ref, sums_ref,
+    shards, part_ref, mid_ref, g_ref, gain_ref, w_ref, a2_ref, dp_ref, act_ref, f2_ref, pw_ref,
+    dm_ref, db_ref, wg_ref, sums_ref, f1g_ref, mlp_ref, do_ref,
     mate, far, outb, sum_sems, share_sems, w_cross, w_line, w_sems,
 ):
     _, _, t = place()
@@ -733,7 +820,13 @@
     gather.forward(0)
     gather.forward(1)
     rows = [jnp.zeros((1, mid_ref.shape[2]), F32) for _ in range(4)]
+    last = collect.pieces - 1
+    grads = f1g_ref.shape[0] // 256
+    tiles = mlp_ref.shape[0] // 256
+    grad_tiles(f1g_ref, a2_ref, dp_ref, 0, grads // 2)
     for p in range(2):
+        if p <= last:
+            collect.step(p)
         unit, inverse = ln_stats(mid_ref[p])
         g = g_ref[p].astype(F32)
         da = gather.result(p)
@@ -744,21 +837,38 @@
         share.push(p, p)
         for k, term in enumerate((da * unit, da, low.astype(F32), g)):
             rows[k] = rows[k] + jnp.sum(term, 0, keepdims=True)
+        if p == 0:
+            grad_tiles(f1g_ref, a2_ref, dp_ref, grads // 2, grads - grads // 2)
     for k in range(4):
         sums_ref[k : k + 1, :] = rows[k]
-    collect.forward()
     for p in range(2):
+        row_tiles(mlp_ref, act_ref, f2_ref, NT, p * tiles // 2, tiles // 2)
+        if p + 2 <= last:
+            collect.step(p + 2)
         share.forward(p, p)
+    for k in range(4, collect.pieces):
+        collect.step(k)
+    group = db_ref.shape[1] * db_ref.shape[2]
     for p in range(2):
         gather.finish(p)
         share.finish(p)
+
+        def one(i, _):
+            rows = db_ref[p, pl.ds(2 * i, 2)].reshape(-1, db_ref.shape[3])
+            at = pl.ds(pl.multiple_of(p * group + i * rows.shape[0], 128), rows.shape[0])
+            do_ref[at, :] = mm(rows, pw_ref[...]).astype(BF16)
+            return 0
+
+        lax.fori_loop(0, db_ref.shape[1] // 2, one, 0)
     collect.finish(wg_ref)
 
 
 def bwd_kernel(
     shards, heads, hd, cols, rows, qb,
     qa_ref, ka_ref, qkv_ref, do_ref, o_ref, lse_ref, tab_ref, hot_ref, part_ref, mid_ref, fb_ref, w_ref,
-    dqkv_ref, rg_ref, out_ref, wg_ref,
+    a1_ref, db_ref, ob_ref, w1_ref,
+    rg_ref, out_ref, wg_ref, da_ref, w1g_ref, qs_ref,
+    dqkv_ref,
     kt_ref, acc_k, acc_v, del_ref, res_ref, mate, far, outb, sum_sems, swap_sems, w_cross, w_line, w_sems,
 ):
     _, me, _ = place()
@@ -817,14 +927,24 @@
         lax.fori_loop(0, tok // qb, blk, 0)
         dqkv_ref[:, k_sl] = (scale * acc_k[...])[:, 0:hd].astype(BF16)
         dqkv_ref[:, v_sl] = acc_v[...][:, 0:hd].astype(BF16)
-        if h == min(1, heads - 1):
-            collect.forward()
+        if h < collect.pieces:
+            collect.step(h)
         if h == min(2, heads - 1):
             for p in range(2):
                 total = mid_ref[p] + gather.result(p) + fb_ref[...]
                 res_ref[p] = total.astype(BF16)
             swap = send(res_ref.at[1 - me], out_ref.at[me], swap_sems, 0, {"ctx": 1 - me})
             out_ref[me] = res_ref[me]
+    wide = dqkv_ref.shape[1]
+    for i in range(tok // 256):
+        at = slice(i * 256, (i + 1) * 256)
+        da_ref[at, :] = mm(dqkv_ref[at, :], w1_ref[:, 0:wide], NT).astype(BF16)
+    for k in range(heads, collect.pieces):
+        collect.step(k)
+    grads = w1g_ref.shape[0] // 256
+    grad_tiles(w1g_ref, a1_ref, dqkv_ref, 0, grads, slice(0, wide))
+    grad_tiles(w1g_ref, db_ref, ob_ref, 0, grads, slice(wide, w1g_ref.shape[1]))
+    qs_ref[...] = jnp.sum(dqkv_ref[...].astype(F32), 0, keepdims=True)
     for p in range(2):
         gather.finish(p)
     collect.finish(wg_ref)
@@ -846,6 +966,8 @@
     first = jnp.zeros((1, x_ref.shape[2]), F32)
     second = jnp.zeros((1, x_ref.shape[2]), F32)
     for p in range(2):
+        if p < collect.pieces:
+            collect.step(p)
         unit, inverse = ln_stats(x_ref[p].astype(F32))
         da = gather.result(p)
         res_ref[p] = (dm_ref[p] + ln_back(unit, inverse, gain_ref[...], da)).astype(BF16)
@@ -859,13 +981,15 @@
     waits = []
     for k, peer in enumerate(({"tp": core_mate(t)}, {"tp": far_mate(t)}, {"ctx": 1 - me})):
         copy = send(held.at[k], got.at[k], small_sems, k, peer)
+        if k + 2 < collect.pieces:
+            collect.step(k + 2)
         copy.wait_recv()
         waits.append(copy)
         held[k + 1] = held[k] + got[k]
     line[s] = held[3]
     for d in range(1, shards):
         waits.append(send(held.at[3], line.at[s], small_sems, 2 + d, {"shard": lax.rem(s + d, shards)}))
-    collect.forward()
+    collect.finish(wg_ref)
     for k, copy in enumerate(waits):
         if k < 3:
             copy.wait_send()
@@ -877,7 +1001,6 @@
     total_ref[...] = acc
     for p in range(2):
         gather.finish(p)
-    collect.finish(wg_ref)
     swap.wait()
 
 
@@ -891,13 +1014,18 @@
 
 
 def position_hots(tok, hd, cols, rows):
-    t = lax.broadcasted_iota(jnp.int32, (tok, 256), 0)
-    l = lax.broadcasted_iota(jnp.int32, (tok, 256), 1)
-    kr = t // cols
-    kw = t % cols
-    first = (l == hd + kr) | (l == hd + rows + kr) | (l == 128 + kw) | (l == 192 + kw)
-    second = (l == hd + rows - 1 - kr) | (l == 128 + cols - 1 - kw)
-    return first.astype(BF16), second.astype(BF16)
+    kr = jnp.arange(rows, dtype=jnp.int32)[:, None]
+    kw = jnp.arange(cols, dtype=jnp.int32)[:, None]
+    l = jnp.arange(256, dtype=jnp.int32)[None, :]
+    first_r = (l == hd + kr) | (l == hd + rows + kr)
+    first_c = (l == 128 + kw) | (l == 192 + kw)
+    second_r = l == hd + rows - 1 - kr
+    second_c = l == 128 + cols - 1 - kw
+
+    def both(r, c):
+        return (r[:, None, :] | c[None, :, :]).astype(BF16).reshape(tok, 256)
+
+    return both(first_r, first_c), both(second_r, second_c)
 
 
 def on_device_images(
@@ -926,7 +1054,7 @@
     fc1_local = lax.dynamic_slice_in_dim(fc1_bias, tp_rank * ff, ff, 0)
     tab_f, tab_b = position_tables(rel_rows, rel_cols, HD)
     hot_f, hot_b = position_hots(tok, HD, COLS, rows)
-    spread = Spread.scratch(shards)
+    spread = Spread.scratch(shards, block)
     collect = Collect.scratch(shards, block)
     gather = Gather2.scratch(piece)
     swap = [DMA((2, 1))]
@@ -946,56 +1074,55 @@
     qkv_full = w1_full[:, :qkv_cols]
     proj_full = w1_full[:, qkv_cols:]
     qkv = (mm(a1, qkv_full) + qkv_bias).astype(BF16)
-    o, o_low, lse, qa, ka, g, cot, fc1_full = comm_call(
+    o, o_low, lse, qa, ka, g, cot, fc1_full, proj_part = comm_call(
         partial(fwd_kernel, shards, heads, HD, COLS, rows, 256), "attn_fwd", 1,
-        (qkv, tab_f, hot_f, cotangent, fc1_weight),
+        (qkv, tab_f, hot_f, cotangent, fc1_weight, proj_full),
         (
             S((tok, width), F32), S((tok, width), BF16), S((heads, tok), F32),
             S((heads, tok, 256), BF16), S((heads, tok, 256), BF16),
-            S(own, BF16), S(full, BF16), S(blocks, BF16),
+            S(own, BF16), S(full, BF16), S(blocks, BF16), S((tok, D), BF16),
         ),
         swap + share + spread, hbm_in=(4,), hbm_out=(7,),
     )
     fc1_full = fc1_full.reshape(D, ff)
     cot = cot.reshape(tok, D)
-    proj_part = mm(o_low, proj_full, NT).astype(BF16).reshape(full)
-    mid, a2, fc2_full = comm_call(
+    proj_part = proj_part.reshape(full)
+    mid, a2, fc2_full, act, slope = comm_call(
         partial(mid_kernel, shards), "mid", 2,
-        (proj_part, x, row(proj_bias), row(norm2_gain), row(norm2_bias), fc2_t),
-        (S(own, F32), S(full, BF16), S(blocks, BF16)),
+        (proj_part, x, row(proj_bias), row(norm2_gain), row(norm2_bias), fc2_t, fc1_full, row(fc1_local)),
+        (S(own, F32), S(full, BF16), S(blocks, BF16), S((tok, ff), BF16), S((tok, ff), F32)),
         gather + share + spread, hbm_in=(5,), hbm_out=(2,),
     )
     a2 = a2.reshape(tok, D)
     fc2_full = fc2_full.reshape(D, ff)
-    pre = mm(a2, fc1_full) + fc1_local
-    cdf = 0.5 * (1.0 + lax.erf(pre * (2.0**-0.5)))
-    act = (pre * cdf).astype(BF16)
-    slope = cdf + pre * jnp.exp(-0.5 * pre * pre) * ((2.0 * math.pi) ** -0.5)
     d_pre = (mm(cot, fc2_full) * slope).astype(BF16)
     d_a2 = mm(d_pre, fc1_full, NT).astype(BF16).reshape(full)
-    fc2_grad = mm(cot, act, TN).astype(BF16).reshape(blocks)
-    d_mid, d_branch, fc2_own, sums = comm_call(
+    fc2_grad = mm(cot, act, TN).astype(BF16)
+    d_mid, d_branch, fc2_own, sums, fc1_grad, mlp_part, d_o = comm_call(
         partial(turn_kernel, shards), "turn", 3,
-        (d_a2, mid, g, row(norm2_gain), fc2_grad),
-        (S(own, F32), S(full, BF16), S(block, F32), S((4, D), F32)),
+        (d_a2, mid, g, row(norm2_gain), fc2_grad, a2, d_pre, act, fc2_full, proj_full),
+        (
+            S(own, F32), S(full, BF16), S(block, F32), S((4, D), F32),
+            S((D, ff), BF16), S((tok, D), BF16), S((tok, width), BF16),
+        ),
         gather + share + collect,
     )
-    fc1_grad = mm(a2, d_pre, TN).astype(BF16).reshape(blocks)
-    mlp_part = mm(act, fc2_full, NT).astype(BF16).reshape(full)
     d_branch = d_branch.reshape(tok, D)
-    d_o = mm(d_branch, proj_full).astype(BF16)
-    dqkv, rel_grad, output, fc1_own = comm_call(
+    mlp_part = mlp_part.reshape(full)
+    rel_grad, output, fc1_own, d_a1, w1_grad, qkv_sum = comm_call(
         partial(bwd_kernel, shards, heads, HD, COLS, rows, 256), "attn_bwd", 4,
-        (qa, ka, qkv, d_o, o, lse, tab_b, hot_b, mlp_part, mid, row(fc2_bias), fc1_grad),
-        (S((tok, qkv_cols), BF16), S((256, 128), F32), S(own, BF16), S(block, F32)),
+        (qa, ka, qkv, d_o, o, lse, tab_b, hot_b, mlp_part, mid, row(fc2_bias), fc1_grad, a1, d_branch, o_low, w1_full),
+        (
+            S((256, 128), F32), S(own, BF16), S(block, F32),
+            S((tok, D), BF16), S((D, qkv_cols + width), BF16), S((1, qkv_cols), F32),
+        ),
         [
-            pltpu.VMEM((256, tok), BF16), pltpu.VMEM((tok, 128), F32), pltpu.VMEM((tok, 128), F32),
+            pltpu.VMEM((tok, qkv_cols), BF16), pltpu.VMEM((256, tok), BF16), pltpu.VMEM((tok, 128), F32), pltpu.VMEM((tok, 128), F32),
             pltpu.VMEM((8, tok), F32), pltpu.VMEM(own, BF16),
         ] + gather + swap + collect,
     )
-    d_a1 = mm(dqkv, qkv_full, NT).astype(BF16).reshape(full)
-    w1_grad = jnp.concatenate([mm(a1, dqkv, TN), mm(d_branch, o_low, TN)], 1).astype(BF16).reshape(blocks)
-    qkv_sum = jnp.sum(dqkv.astype(F32), 0)
+    d_a1 = d_a1.reshape(full)
+    qkv_sum = qkv_sum[0]
     qv_part = jnp.stack([qkv_sum[:width], qkv_sum[2 * width :]])
     qv_placed = lax.dynamic_update_slice_in_dim(jnp.zeros((2, D), F32), qv_part, tp_rank * width, 1)
     fc1_sum = jnp.sum(d_pre.astype(F32), 0)

time: 510 us -> 406 us (0.80)
  Pallas kernels: 404 us -> 346 us
  matrix products: 61.4 us -> 22.6 us
  other arithmetic: 9.59 us -> 4.45 us
    pallas_call x6, Pallas kernels: 404 us -> 346 us  [comm_call(): pl.pallas_call(kernel, out_shape=tuple(outs), in_specs=[ANY if i in hbm_i...]
    dot_general x12 -> x4, matrix products: 61.4 us -> 22.6 us  [mm(): return lax.dot_general(left, right, dims, preferred_element_type=F32)]
    dot_general x2 -> x0, local copies, waits for them, and re-layouts: 5.62 us -> none  [mm(): return lax.dot_general(left, right, dims, preferred_element_type=F32)]
where the time goes in v3:
time: 406 us; the launch traced here: 401 us
  Pallas kernels  346 us (85%)
  local copies, waits for them, and re-layouts  26.1 us (6%)
  matrix products  22.6 us (6%)
  other arithmetic  4.45 us (1%)
    pallas_call x6, Pallas kernels, comm_call(): pl.pallas_call(kernel, out_shape=tuple(outs), in_specs=[ANY if i in hbm_i...  346 us
    dot_general x4, matrix products, mm(): return lax.dot_general(left, right, dims, preferred_element_type=F32)  22.6 us

profile of v3, /device:TPU:8, one launch (start us, length us, event | category | flops | bytes accessed | tf_op | source)
XLA Modules:
  0.0 400.5 jit_solution(2320323295321516910)
XLA Ops:
  0.6 0.9 dynamic-slice_reduce_fusion.1
  1.6 1.1 slice_bitcast_fusion.4
  2.7 1.9 concatenate.15.w_ref
  4.5 1.3 reshape.272.gain_ref
  5.8 1.3 reshape.273.bias_ref
  7.1 50.3 %front.1 = (bf16[2,128,1280]{2,1,0:T(8,128)(2,1)}, bf16[2,4,128,1280]{3,2,1,0:T(8,128)(2,1)}, bf16[8,160,1280]{2,1,0:T(8,128)(2,1)}) custom-call(bf16[2,128,1280]{2,1,0:T(8,128)(2,1)} %tok_ref.1, bf16[160,1280]{1,0:T(8,128)(2,1)} %concatenate.15.w_ref, f32[1,1280]{1,0:T(1,128)} %reshape.272.gain_ref, f32[1,1280]{1,0:T(1,128)} %reshape.273.bias_ref), custom_call_target="tpu_custom_call" | custom-call | tf_op jit(solution)/shard_map/front/pallas_call | solution.py:638
  57.4 6.8 %add_convert_fusion.qkv_ref = bf16[1024,960]{1,0:T(8,128)(2,1)} fusion(f32[960]{0:T(1024)S(1)} %pad_maximum_fusion.1, bf16[1024,1280]{1,0:T(8,128)(2,1)} %bitcast.46, bf16[1280,1280]{1,0:T(8,128)(2,1)} %bitcast.39), kind=kOutput, calls=%fused_computation.3 | convolution fusion | flops 2518548480 | bytes 7212800 | tf_op jit(solution)/shard_map/dot_general | solution.py:388
  64.2 2.6 slice.128.pw_ref
  67.0 0.9 or_convert_fusion.1
  68.9 57.1 %attn_fwd.1 = (f32[1024,320]{1,0:T(8,128)}, bf16[1024,320]{1,0:T(8,128)(2,1)}, f32[4,1024]{1,0:T(4,128)}, bf16[4,1024,256]{2,1,0:T(8,128)(2,1)}, bf16[4,1024,256...) custom-call(bf16[1024,960]{1,0:T(8,128)(2,1)} %add_convert_fusion.qk, ...), custom_call_target="tpu_custom_call" | custom-call | tf_op jit(solution)/shard_map/attn_fwd/pallas_call | solution.py:638
  129.2 51.0 %mid.1 = (f32[2,128,1280]{2,1,0:T(8,128)}, bf16[2,4,128,1280]{3,2,1,0:T(8,128)(2,1)}, bf16[8,160,1280]{2,1,0:T(8,128)(2,1)}, bf16[1024,1280]{1,0:T(8,128)(2,1)}, f32[1024,1280]{1,0:T(8,128)}) custom-call(bf16[2,4,128,1280]{3,2,1,0:T(8,128)(2,1)} %bitcast.51, bf16[2,128,1280]{2,1,0:T(8,128)(2,1)} %get-tuple-element.55.x_ref, f32[1,1280]{1,0:T(1,128)} %reshape.278.pb_ref, ...), custom_call_target="tpu_custom_call" | custom-call | tf_op jit(solution)/shard_map/mid/pallas_call | solution.py:638
  180.2 7.1 %convolution_convert_fusion.w_ref = bf16[1280,1280]{1,0:T(8,128)(2,1)} fusion(bf16[1024,1280]{1,0:T(8,128)(2,1)S(1)} %bitcast.59, bf16[1024,1280]{1,0:T(8,128)(2,1)} %get-tuple-element.61.act_ref), kind=kOutput, calls=%fused_computation | convolution fusion | flops 3357081600 | bytes 8519680 | tf_op jit(solution)/shard_map/dot_general | solution.py:388
  187.3 3.8 convert_reduce_fusion
  191.1 4.9 %convolution_convert_fusion.1 = bf16[1024,1280]{1,0:T(8,128)(2,1)} fusion(bf16[1024,1280]{1,0:T(8,128)(2,1)S(1)} %get-tuple-element.116.dp_ref, bf16[1280,1280]{1,0:T(8,128)(2,1)S(1)} %bitcast.43), kind=kOutput, calls=%fused_computation.4 | convolution fusion | flops 3356753920 | bytes 8519680 | tf_op jit(solution)/shard_map/dot_general | solution.py:388
  196.0 60.8 %turn.1 = (f32[2,128,1280]{2,1,0:T(8,128)}, bf16[2,4,128,1280]{3,2,1,0:T(8,128)(2,1)}, f32[160,1280]{1,0:T(8,128)}, f32[4,1280]{1,0:T(4,128)}, bf16[1280,1280]{1...) custom-call(bf16[2,4,128,1280]{3,2,1,0:T(8,128)(2,1)} %bitcast.53, ...), custom_call_target="tpu_custom_call" | custom-call | tf_op jit(solution)/shard_map/turn/pallas_call | solution.py:638
  257.0 0.9 or_convert_fusion
  259.3 61.3 %attn_bwd.1 = (f32[256,128]{1,0:T(8,128)}, bf16[2,128,1280]{2,1,0:T(8,128)(2,1)}, f32[160,1280]{1,0:T(8,128)}, bf16[1024,1280]{1,0:T(8,128)(2,1)}, bf16[1280,1280]{1,0:T(8,128)(2,1)}, /*index=5*/f32[1,960]{1,0:T(1,128)}) custom-call(bf16[4,1024,256]{2,1,0:T(8,128)(2,1)} %get-tuple-element.51.qa_ref, bf16[4,1024,256]{2,1,0:T(8,128)(2,1)} %get-tuple-element.52.ka_ref, ...), custom_call_target="tpu_custom_call" | custom-call | tf_op jit(solution)/shard_map/attn_bwd/pallas_call | solution.py:638
  321.5 0.8 slice.106
  324.4 65.8 %end.1 = (bf16[2,128,1280]{2,1,0:T(8,128)(2,1)}, f32[160,1280]{1,0:T(8,128)}, f32[24,1280]{1,0:T(8,128)}) custom-call(bf16[2,4,128,1280]{3,2,1,0:T(8,128)(2,1)} %bitcast.50, bf16[2,128,1280]{2,1,0:T(8,128)(2,1)} %get-tuple-element.55.x_ref, f32[2,128,1280]{2,1,0:T(8,128)} %get-tuple-element.72.dm_ref, f32[1,1280]{1,0:T(1,128)} %reshape.272.gain_ref, ...), custom_call_target="tpu_custom_call" | custom-call | tf_op jit(solution)/shard_map/end/pallas_call | solution.py:638
  390.3 2.3 slice_bitcast_fusion
  392.6 0.9 pad_maximum_fusion
  396.9 0.8 copy.47
  398.5 0.9 copy.49
  399.4 0.9 copy.50
  (82 shorter events, 13.1 us)
Async XLA Ops:
  57.4 10.5 %copy-start.9 = (bf16[31,80]{1,0:T(8,128)(2,1)S(1)}, bf16[31,80]{1,0:T(8,128)(2,1)}, u32[]{:S(2)}) copy-start(bf16[31,80]{1,0:T(8,128)(2,1)} %param.21) | copy-start | bytes 14884
  64.2 3.9 copy-start.8
  67.9 59.4 %copy-start.11 = (f32[1280]{0:T(1024)S(1)}, f32[1280]{0:T(1024)}, u32[]{:S(2)}) copy-start(f32[1280]{0:T(1024)} %param.25) | copy-start | bytes 15364
  67.9 60.0 %copy-start.12 = (f32[1280]{0:T(1024)S(1)}, f32[1280]{0:T(1024)}, u32[]{:S(2)}) copy-start(f32[1280]{0:T(1024)} %param.24) | copy-start | bytes 15364
  67.9 60.6 %copy-start.13 = (f32[1280]{0:T(1024)S(1)}, f32[1280]{0:T(1024)}, u32[]{:S(2)}) copy-start(f32[1280]{0:T(1024)} %param.26) | copy-start | bytes 15364
  129.2 51.0 %copy-start.16 = (bf16[2,4,128,1280]{3,2,1,0:T(8,128)(2,1)S(1)}, bf16[2,4,128,1280]{3,2,1,0:T(8,128)(2,1)}, u32[]{:S(2)}) copy-start(bf16[2,4,128,1280]{3,2,1,0:T(8,128)(2,1)} %get-tuple-element.53) | copy-start | bytes 7864324
  180.2 7.2 %copy-start.1 = (bf16[8,160,1280]{2,1,0:T(8,128)(2,1)S(1)}, bf16[8,160,1280]{2,1,0:T(8,128)(2,1)}, u32[]{:S(2)}) copy-start(bf16[8,160,1280]{2,1,0:T(8,128)(2,1)} %get-tuple-element.57) | copy-start | bytes 9830404
  180.2 7.2 %copy-start.15 = (f32[1024,1280]{1,0:T(8,128)S(1)}, f32[1024,1280]{1,0:T(8,128)}, u32[]{:S(2)}) copy-start(f32[1024,1280]{1,0:T(8,128)} %get-tuple-element.58) | copy-start | bytes 15728644
  180.2 7.1 %copy-start.17 = (bf16[2,4,128,1280]{3,2,1,0:T(8,128)(2,1)S(1)}, bf16[2,4,128,1280]{3,2,1,0:T(8,128)(2,1)}, u32[]{:S(2)}) copy-start(bf16[2,4,128,1280]{3,2,1,0:T(8,128)(2,1)} %get-tuple-element.53) | copy-start | bytes 7864324
  187.3 3.8 copy-start
  191.1 4.9 %copy-start.2 = (bf16[1024,1280]{1,0:T(8,128)(2,1)}, bf16[1024,1280]{1,0:T(8,128)(2,1)S(1)}, u32[]{:S(2)}) copy-start(bf16[1024,1280]{1,0:T(8,128)(2,1)S(1)} %get-tuple-element.116.dp_ref) | copy-start | bytes 7864324
  196.0 62.7 %copy-start.14 = (f32[1280]{0:T(1024)S(1)}, f32[1280]{0:T(1024)}, u32[]{:S(2)}) copy-start(f32[1280]{0:T(1024)} %param.30) | copy-start | bytes 15364
  259.3 64.0 %copy-start.10 = (f32[4,1280]{1,0:T(4,128)S(1)}, f32[4,1280]{1,0:T(4,128)}, u32[]{:S(2)}) copy-start(f32[4,1280]{1,0:T(4,128)} %get-tuple-element.75) | copy-start | bytes 61444
  390.3 3.2 copy-start.7
  390.3 6.6 %copy-start.5 = (bf16[2,128,1280]{2,1,0:T(8,128)(2,1)S(1)}, bf16[2,128,1280]{2,1,0:T(8,128)(2,1)}, u32[]{:S(2)}) copy-start(bf16[2,128,1280]{2,1,0:T(8,128)(2,1)} %get-tuple-element.137) | copy-start | bytes 1966084
  390.3 7.4 %copy-start.6 = (bf16[2,128,1280]{2,1,0:T(8,128)(2,1)S(1)}, bf16[2,128,1280]{2,1,0:T(8,128)(2,1)}, u32[]{:S(2)}) copy-start(bf16[2,128,1280]{2,1,0:T(8,128)(2,1)} %get-tuple-element.138) | copy-start | bytes 1966084
  392.6 6.0 %copy-start.4 = (f32[160,1280]{1,0:T(8,128)S(1)}, f32[160,1280]{1,0:T(8,128)}, u32[]{:S(2)}) copy-start(f32[160,1280]{1,0:T(8,128)} %get-tuple-element.149) | copy-start | bytes 2457604
  393.5 6.0 %copy-start.3 = (f32[160,1280]{1,0:T(8,128)S(1)}, f32[160,1280]{1,0:T(8,128)}, u32[]{:S(2)}) copy-start(f32[160,1280]{1,0:T(8,128)} %get-tuple-element.81) | copy-start | bytes 2457604
